TPU v7x, 256 devices: a whole 4x4x8 slice. The times are simulated.
256 devices in a mesh: dir: 32 (over z, x), coil: 8 (over y, core).
Axes of the slice: x: 4, y: 4, z: 8, core: 2. Of those that a mesh axis runs over, the one named last changes fastest.
Arguments:
- kspace: bfloat16 [64, 8, 32, 128, 512], P(None, None, 'coil', 'dir'), may hold values from -6 to 6
- accept: int32 [64, 8], replicated, may hold values from 0 to 1, as said below
- trajectory: int32 [64, 8, 128], P('dir'), may hold values from 0 to 255
- phase_coef: float32 [64, 8, 16, 16], P('dir'), may hold values from -2 to 2
- sens: bfloat16 [32, 256, 512], P('coil'), may hold values from -1.1953125 to 1.1953125
Outputs:
- image: float32 [64, 256, 512], P('dir', 'coil')
Inputs may be any that keep to these rules, and one draw needn't show every extreme that they name: `accept`: each direction accepts 1 to 6 of its 8 shots, and some direction accepts exactly 6.
All inputs are finite; a program needn't handle non-finite values.
Results may differ from a plain program's by a relative error of at most 0.0043.
Values may be sent and summed in bfloat16 or wider, within the bound.
A program may use at most 128 MiB of HBM per device.

v0:
```python
import math

import jax
import jax.numpy as jnp
from jax import lax
from jax.sharding import PartitionSpec as P

IMG = 256
SHOTS = 8
ACCEPTED = 6
PB = 16


def readout_table(size):
    points = jnp.arange(size, dtype=jnp.int32)
    product = points[:, None] * points[None, :] % size
    angles = product.astype(jnp.float32) * (2.0 * math.pi / size)
    cosine = jnp.cos(angles)
    sine = jnp.sin(angles)
    upper = jnp.concatenate([cosine, sine], 1)
    lower = jnp.concatenate([-sine, cosine], 1)
    return jnp.concatenate([upper, lower], 0).astype(jnp.bfloat16)


def line_tables(ky_lines, size):
    points = jnp.arange(size, dtype=jnp.int32)
    product = ky_lines[:, None] * points[None, :] % size
    angles = product.astype(jnp.float32) * (2.0 * math.pi / size)
    return (jnp.cos(angles).astype(jnp.bfloat16), jnp.sin(angles).astype(jnp.bfloat16))


def cosine_basis(size, terms):
    points = jnp.arange(size, dtype=jnp.int32).astype(jnp.float32)
    orders = jnp.arange(terms, dtype=jnp.int32).astype(jnp.float32)
    return jnp.cos(math.pi * orders[None, :] * (points[:, None] + 0.5) / size)


def shot_image(shot_data, ky_lines, readout_tab, sens):
    coils, row_count, width = shot_data.shape
    halfwidth = width // 2
    spectra = jnp.dot(
        shot_data.reshape(coils * row_count, width), readout_tab, preferred_element_type=jnp.float32
    )
    spectra = (
        (spectra * (1.0 / math.sqrt(halfwidth)))
        .astype(jnp.bfloat16)
        .reshape(coils, row_count, width)
    )
    swapped = jnp.concatenate([-spectra[..., halfwidth:], spectra[..., :halfwidth]], -1)
    cos_tab, sin_tab = line_tables(ky_lines, halfwidth)
    coil_images = jnp.einsum("ry,crx->cyx", cos_tab, spectra, preferred_element_type=jnp.float32)
    coil_images = coil_images + jnp.einsum(
        "ry,crx->cyx", sin_tab, swapped, preferred_element_type=jnp.float32
    )
    coil_images = coil_images * (1.0 / math.sqrt(row_count))
    sens_re = sens[..., :halfwidth].astype(jnp.float32)
    sens_im = sens[..., halfwidth:].astype(jnp.float32)
    image_re = coil_images[..., :halfwidth]
    image_im = coil_images[..., halfwidth:]
    unit_re = jnp.sum(sens_re * image_re + sens_im * image_im, 0)
    unit_im = jnp.sum(sens_re * image_im - sens_im * image_re, 0)
    return jnp.concatenate([unit_re, unit_im], -1)


def phase_apply(images, coefs, weights, basis_rows, basis_cols):
    halfwidth = images.shape[2] // 2
    partial_map = jnp.einsum("yk,skl->syl", basis_rows, coefs, precision=lax.Precision.HIGHEST)
    angles = jnp.einsum("syl,xl->syx", partial_map, basis_cols, precision=lax.Precision.HIGHEST)
    cosine = jnp.cos(angles)
    sine = jnp.sin(angles)
    unit_re = images[..., :halfwidth]
    unit_im = images[..., halfwidth:]
    scaled = weights.astype(jnp.float32)[:, None, None]
    out_re = jnp.sum(scaled * (cosine * unit_re + sine * unit_im), 0) / SHOTS
    out_im = jnp.sum(scaled * (cosine * unit_im - sine * unit_re), 0) / SHOTS
    return jnp.concatenate([out_re, out_im], -1)


def on_device(kspace, accept, trajectory, phase_coef, sens):
    dir_index = lax.axis_index("dir")
    coil_index = lax.axis_index("coil")
    coil_count = lax.axis_size("coil")
    owned = trajectory.shape[0]
    own_accept = lax.dynamic_slice_in_dim(accept, dir_index * owned, owned, 0)
    shot_order = jnp.argsort(1 - accept, axis=1, stable=True)[:, :ACCEPTED]
    picked = jnp.take_along_axis(kspace, shot_order[:, :, None, None, None], axis=1)
    blocks = lax.all_to_all(picked, "dir", split_axis=0, concat_axis=3, tiled=True)
    own_order = lax.dynamic_slice_in_dim(shot_order, dir_index * owned, owned, 0)
    weights = jnp.take_along_axis(own_accept, own_order, axis=1)
    ky_rows = jnp.take_along_axis(trajectory, own_order[:, :, None], axis=1)
    coefs = jnp.take_along_axis(phase_coef, own_order[:, :, None, None], axis=1)
    shot_count = weights.shape[1]
    readout_tab = readout_table(IMG)
    flat_blocks = blocks.reshape((owned * shot_count,) + blocks.shape[2:])
    flat_lines = ky_rows.reshape(owned * shot_count, ky_rows.shape[2])
    images = lax.map(
        lambda pair: shot_image(pair[0], pair[1], readout_tab, sens), (flat_blocks, flat_lines)
    )
    images = images.reshape(owned, shot_count, IMG, 2 * IMG)
    basis_full = cosine_basis(IMG, PB)
    row_count = IMG // coil_count
    shared = lax.psum_scatter(images, "coil", scatter_dimension=2, tiled=True)
    basis_mine = lax.dynamic_slice_in_dim(basis_full, coil_index * row_count, row_count, 0)
    return jax.vmap(
        lambda shots_img, shot_coefs, shot_flags: phase_apply(
            shots_img, shot_coefs, shot_flags, basis_mine, basis_full
        )
    )(shared, coefs, weights)


def solution(mesh):
    return jax.shard_map(
        on_device,
        mesh=mesh,
        in_specs=(
            P(None, None, "coil", "dir", None),
            P(),
            P("dir", None, None),
            P("dir", None, None, None),
            P("coil", None, None),
        ),
        out_specs=P("dir", "coil", None),
        check_vma=False,
    )
```

profile of v0, /device:TPU:1, one launch (start us, length us, event | category | flops | bytes accessed | tf_op | source)
XLA Modules:
  0.0 326.9 jit_solution(17845313448420577109)
XLA Ops:
  6.5 0.7 broadcast_subtract_fusion
  7.3 0.7 sort.17
  8.3 21.5 %gather_fusion.2 = bf16[384,4,4,512]{3,2,1,0:T(4,128)(2,1)} fusion(bf16[64,8,4,4,512]{4,3,2,1,0:T(4,128)(2,1)} %param.7, s32[384]{0:T(512)S(1)} %reshape.114), kind=kCustom, calls=%fused_computation.2 | custom fusion | bytes 12585984 | tf_op jit(solution)/shard_map/jit(take_along_axis)/gather | solution.py:86
  29.7 8.5 %broadcast_select_fusion = bf16[64,6,4,4,512]{4,3,2,1,0:T(4,128)(2,1)} fusion(bf16[64,6,4,4,512]{4,3,2,1,0:T(4,128)(2,1)} %bitcast.70, pred[64,6]{1,0:T(8,128)(4,1)S(1)} %copy.43), kind=kLoop, calls=%fused_computation.46 | loop fusion | flops 3145728 | bytes 12583296 | tf_op jit(solution)/shard_map/jit(take_along_axis)/select_n | solution.py:86
  38.3 12.1 %all-to-all-start = ((bf16[64,6,4,4,512]{4,3,2,1,0:T(4,128)(2,1)}), bf16[64,6,4,4,512]{4,3,2,1,0:T(4,128)(2,1)}, u32[]{:S(2)}, u32[]{:S(2)}) async-start(bf16[64,6,4,4,512]{4,3,2,1,0:T(4,128)(2,1)} %broadcast_select_fusion), calls=%async_computation | async-start | bytes 12582912 | tf_op jit(solution)/shard_map/all_to_all | solution.py:87
  51.0 0.7 gather_fusion
  52.1 0.6 gather_fusion.3
  53.3 1.0 fusion.38
  54.3 1.1 negate_convert_fusion
  55.5 131.9 %all-to-all-done = bf16[64,6,4,4,512]{4,3,2,1,0:T(4,128)(2,1)} async-done(((bf16[64,6,4,4,512]{4,3,2,1,0:T(4,128)(2,1)}), bf16[64,6,4,4,512]{4,3,2,1,0:T(4,128)(2,1)}, u32[]{:S(2)}, u32[]{:S(2)}) %all-to-all-start) | async-done | bytes 6291488 | tf_op jit(solution)/shard_map/all_to_all | solution.py:87
  187.4 10.1 %copy.45 = bf16[2,6,4,32,4,512]{5,2,4,3,1,0:T(4,128)(2,1)} copy(bf16[2,6,4,32,4,512]{5,4,2,1,0,3:T(4,128)(2,1)} %bitcast.17) | data formatting | bytes 12582912 | tf_op jit(solution)/shard_map/all_to_all | solution.py:87
  197.5 68.2 %while.12 = (s32[]{:T(128)}, f32[12,256,512]{2,1,0:T(8,128)}, bf16[4,256,512]{1,2,0:T(8,128)(2,1)S(1)}, bf16[12,4,128,512]{3,1,2,0:T(4,128)(2,1)}, bf16[512,512]...) while((s32[]{:T(128)}, f32[12,256,512]{2,1,0:T(8,128)}, bf16[4,256,512]{1,2,0:T(8,128)(2,1)S(1)}, ...), condition=%wide.region_4.5_spmd, body=%wide.region_1.4_spmd.sunk | while | flops 543227904 | bytes 20449376 | solution.py:96
  197.6 1.2 constant_dynamic-slice_fusion.4
  199.8 1.0 fusion.74
  200.7 1.0 multiply_bitcast_fusion.2
  202.4 0.8 constant_dynamic-update-slice_fusion.2
  203.2 1.2 constant_dynamic-slice_fusion.4
  205.5 1.0 fusion.74
  206.4 1.0 multiply_bitcast_fusion.2
  208.1 0.9 constant_dynamic-update-slice_fusion.2
  208.9 1.2 constant_dynamic-slice_fusion.4
  211.2 1.0 fusion.74
  212.1 1.0 multiply_bitcast_fusion.2
  213.7 0.8 constant_dynamic-update-slice_fusion.2
  214.6 1.2 constant_dynamic-slice_fusion.4
  216.8 1.0 fusion.74
  217.8 1.0 multiply_bitcast_fusion.2
  219.4 0.9 constant_dynamic-update-slice_fusion.2
  220.3 1.2 constant_dynamic-slice_fusion.4
  222.5 1.0 fusion.74
  223.5 1.0 multiply_bitcast_fusion.2
  225.1 0.9 constant_dynamic-update-slice_fusion.2
  226.0 1.2 constant_dynamic-slice_fusion.4
  228.2 1.0 fusion.74
  229.2 1.0 multiply_bitcast_fusion.2
  230.8 0.9 constant_dynamic-update-slice_fusion.2
  231.7 1.2 constant_dynamic-slice_fusion.4
  234.0 1.0 fusion.74
  234.9 1.0 multiply_bitcast_fusion.2
  236.5 0.8 constant_dynamic-update-slice_fusion.2
  237.4 1.2 constant_dynamic-slice_fusion.4
  239.6 1.0 fusion.74
  240.6 1.0 multiply_bitcast_fusion.2
  242.2 0.8 constant_dynamic-update-slice_fusion.2
  243.0 1.2 constant_dynamic-slice_fusion.4
  245.3 1.0 fusion.74
  246.2 1.0 multiply_bitcast_fusion.2
  247.9 0.9 constant_dynamic-update-slice_fusion.2
  248.7 1.2 constant_dynamic-slice_fusion.4
  251.0 1.0 fusion.74
  251.9 1.0 multiply_bitcast_fusion.2
  253.6 0.9 constant_dynamic-update-slice_fusion.2
  254.4 1.2 constant_dynamic-slice_fusion.4
  256.7 1.0 fusion.74
  257.6 1.0 multiply_bitcast_fusion.2
  259.2 0.8 constant_dynamic-update-slice_fusion.2
  260.1 1.2 constant_dynamic-slice_fusion.4
  262.3 1.0 fusion.74
  263.3 1.0 multiply_bitcast_fusion.2
  264.9 0.8 constant_dynamic-update-slice_fusion.2
  267.1 1.9 fusion.50
  269.0 49.1 %reduce-scatter.2.cloned.1.call-done = f32[2,6,32,512]{3,2,1,0:T(8,128)} async-done(((f32[2,6,256,512]{3,2,1,0:T(8,128)}), f32[2,6,32,512]{3,2,1,0:T(8,128)}) %reduce-scatter.2.cloned.1.call-update) | async-done | bytes 786448 | tf_op jit(solution)/shard_map/reduce_scatter | solution.py:102
  318.1 1.3 multiply_reduce_fusion.1
  319.4 0.7 pad_maximum_fusion
  (159 shorter events, 22.5 us)
Async XLA Ops:
  6.5 259.4 %copy-start = (f32[2,8,16,16]{3,2,1,0:T(8,128)S(1)}, f32[2,8,16,16]{3,2,1,0:T(8,128)}, u32[]{:S(2)}) copy-start(f32[2,8,16,16]{3,2,1,0:T(8,128)} %param.10) | copy-start | bytes 49156
  38.3 12.6 %copy-start.3 = (s32[64,8]{0,1:T(8,128)S(1)}, s32[64,8]{0,1:T(8,128)}, u32[]{:S(2)}) copy-start(s32[64,8]{0,1:T(8,128)} %param.8) | copy-start | bytes 6148
  38.3 13.8 %copy-start.2 = (s32[2,8,128]{2,1,0:T(8,128)S(1)}, s32[2,8,128]{2,1,0:T(8,128)}, u32[]{:S(2)}) copy-start(s32[2,8,128]{2,1,0:T(8,128)} %param.9) | copy-start | bytes 24580
  38.3 14.5 %copy-start.1 = (bf16[4,256,512]{2,1,0:T(8,128)(2,1)S(1)}, bf16[4,256,512]{2,1,0:T(8,128)(2,1)}, u32[]{:S(2)}) copy-start(bf16[4,256,512]{2,1,0:T(8,128)(2,1)} %param.11) | copy-start | bytes 3145732
  38.3 149.2 %all-to-all-start = ((bf16[64,6,4,4,512]{4,3,2,1,0:T(4,128)(2,1)}), bf16[64,6,4,4,512]{4,3,2,1,0:T(4,128)(2,1)}, u32[]{:S(2)}, u32[]{:S(2)}) async-start(bf16[64,6,4,4,512]{4,3,2,1,0:T(4,128)(2,1)} %broadcast_select_fusion), calls=%async_computation | async-start | bytes 12582912 | tf_op jit(solution)/shard_map/all_to_all | solution.py:87
  50.4 267.7 %reduce-scatter.2.cloned.1.call-start = ((), (), s32[]{:S(2)}) async-start(), calls=%async_computation.2 | async-start | bytes 7077888 | tf_op jit(solution)/shard_map/reduce_scatter | solution.py:102
Sparse Core Ops, SparseCore 0:
  265.9 52.1 reduce-scatter.1
where the time goes:
time: 328 us; the launch traced here: 327 us
  waiting for transfers between devices  181 us (55%)
  local copies, waits for them, and re-layouts  68.2 us (21%)
  matrix products  30.6 us (9%)
  other arithmetic  20.3 us (6%)
  between operations  13.5 us (4%)
  starting transfers between devices  12.3 us (4%)
    all_to_all x1, waiting for transfers between devices, on_device(): lax.all_to_all(picked, 'dir', split_axis=0, concat_axis=3, tiled=True)  132 us
    reduce_scatter x1, waiting for transfers between devices, on_device(): shared = lax.psum_scatter(images, 'coil', scatter_dimension=2, tiled=True)  49.1 us
    gather x3, local copies, waits for them, and re-layouts, on_device(): jnp.take_along_axis(kspace, shot_order[:, :, None, None, None], axis=1)  21.7 us
    dynamic_slice x24, local copies, waits for them, and re-layouts, on_device(): lax.map(lambda pair: shot_image(pair[0], pair[1], readout_tab, sens), (fl...  15.8 us
    dynamic_update_slice x24, local copies, waits for them, and re-layouts, on_device(): lax.map(lambda pair: shot_image(pair[0], pair[1], readout_tab, sens), (fl...  12.6 us
    all_to_all x1, starting transfers between devices, on_device(): lax.all_to_all(picked, 'dir', split_axis=0, concat_axis=3, tiled=True)  12.1 us
    dot_general x12, matrix products, shot_image(): jnp.einsum('ry,crx->cyx', cos_tab, spectra, preferred_element_type=jnp.fl...  11.6 us
    dot_general x12, matrix products, shot_image(): jnp.einsum('ry,crx->cyx', sin_tab, swapped, preferred_element_type=jnp.fl...  11.6 us
  transfers between devices with their start and end apart: 2, of which 2 were waited for; matrix products, arithmetic and copies ran while one was open for 2% of the time, Pallas kernels for 0%

commit v1 on v0

v1 whole, which is shorter than its diff:
```python
import functools
import math

import jax
import jax.numpy as jnp
import numpy as np
from jax import lax
from jax.experimental import pallas as pl
from jax.experimental.pallas import tpu as pltpu
from jax.sharding import Mesh, PartitionSpec as P

IMG = 256
SHOTS = 8
PB = 16
DIRS = 64
HALF = IMG // 2
MESH = pl.DeviceIdType.MESH
AXES = ("zh", "zl", "x", "y", "core")
BF = jnp.bfloat16
F32 = jnp.float32

LEVELS = (32, 36, 40, 48)
STEP = {32: 16, 36: 18, 40: 20, 48: 16}


def readout_const():
    k = np.arange(IMG)
    ang = (np.outer(k, k) % IMG).astype(np.float64) * (2.0 * np.pi / IMG)
    c, s = np.cos(ang).astype(np.float32), np.sin(ang).astype(np.float32)
    tab = np.concatenate([np.concatenate([c, s], 1), np.concatenate([-s, c], 1)], 0)
    order = np.concatenate([np.arange(HALF), IMG + np.arange(HALF), HALF + np.arange(HALF), IMG + HALF + np.arange(HALF)])
    return jnp.asarray(tab[:, order]).astype(BF)


def line_const():
    k = np.arange(IMG)
    ang = (np.outer(k, k) % IMG).astype(np.float64) * (2.0 * np.pi / IMG)
    return jnp.asarray(np.concatenate([np.cos(ang), np.sin(ang)], 1).astype(np.float32)).astype(BF)


def basis_const():
    points = np.arange(IMG, dtype=np.float64)
    orders = np.arange(PB, dtype=np.float64)
    return np.cos(np.pi * orders[None, :] * (points[:, None] + 0.5) / IMG)


def split3(a):
    one = np.asarray(a, np.float32).astype(BF)
    rest = np.asarray(a, np.float64) - one.astype(np.float64)
    two = rest.astype(np.float32).astype(BF)
    rest = rest - two.astype(np.float64)
    return one, two, rest.astype(np.float32).astype(BF)


def poly_consts():
    u = np.cos(np.linspace(0, np.pi, 4001)) * 0.125 + 0.125
    t = np.sqrt(np.maximum(u, 0))
    fs = np.where(t > 1e-9, np.sin(2 * np.pi * t) / np.where(t > 1e-9, t, 1), 2 * np.pi)
    return [float(v) for v in np.polyfit(u, fs, 5)], [float(v) for v in np.polyfit(u, np.cos(2 * np.pi * t), 6)]


SIN_C, COS_C = poly_consts()


def sincos_turns(turns):
    t = turns - jnp.round(turns)
    u = t * t
    s = jnp.full_like(u, SIN_C[0])
    for v in SIN_C[1:]:
        s = s * u + v
    c = jnp.full_like(u, COS_C[0])
    for v in COS_C[1:]:
        c = c * u + v
    return s * t, c


def readout_kernel(count, idx_ref, tab_ref, *refs):
    out_ref = refs[count]
    rows = jnp.concatenate([refs[i][0] for i in range(count)], 0)
    spec = jnp.dot(rows, tab_ref[...], preferred_element_type=F32) * (1.0 / math.sqrt(IMG))
    spec = spec.astype(BF).reshape(count, 16, 2 * IMG)
    out_ref[0, 0, 0] = spec[:, :, :IMG]
    out_ref[0, 1, 0] = spec[:, :, IMG:]


def readout(slots, kspace, index, tab):
    count = STEP[slots]

    def pick(i, q, p, b, idx):
        return (idx[((q * 2 + p) * (slots // count) + b) * count + i], 0, 0)

    return pl.pallas_call(
        functools.partial(readout_kernel, count),
        grid_spec=pltpu.PrefetchScalarGridSpec(
            num_scalar_prefetch=1,
            grid=(4, 2, slots // count),
            in_specs=[pl.BlockSpec((2 * IMG, 2 * IMG), lambda q, p, b, idx: (0, 0))]
            + [pl.BlockSpec((1, 16, 2 * IMG), functools.partial(pick, i)) for i in range(count)],
            out_specs=pl.BlockSpec((1, 2, 1, count, 16, IMG), lambda q, p, b, idx: (q, 0, p, b, 0, 0)),
        ),
        out_shape=jax.ShapeDtypeStruct((4, 2, 2, slots, 16, IMG), BF),
        cost_estimate=pl.CostEstimate(flops=8 * slots * 16 * 512 * 512 * 2, bytes_accessed=8 * slots * 16 * 512 * 4, transcendentals=0),
        name="readout",
    )(index, tab, *([kspace] * count))


def partner(p, i, n):
    if p == 0:
        return i + 1 - 2 * lax.rem(i, 2)
    return lax.rem(i + 2 * lax.rem(i, 2) - 1 + n, n)


def exchange_kernel(slots, send_ref, sens_ref, recv_ref, both_ref, keep, keep_sens, send_sem, recv_sem, local_sem):
    zh, zl = lax.axis_index("zh"), lax.axis_index("zl")
    x, y, core = lax.axis_index("x"), lax.axis_index("y"), lax.axis_index("core")
    z = zh * 2 + zl
    src = lax.rem(x, 2) * 2 + zl

    def target(p, bits):
        bx, bz, bc = bits
        tx = partner(p, x, 4) if bx else x
        tz = partner(p, z, 8) if bz else z
        tc = 1 - core if bc else core
        return tz, tx, tc

    def device(p, bits):
        tz, tx, tc = target(p, bits)
        return (tz // 2, lax.rem(tz, 2), tx, y, tc)

    every = [(p, (bx, bz, bc)) for bx in (1, 0) for bz in (1, 0) for bc in (0, 1) for p in (0, 1) if bx + bz + bc]
    barrier = pltpu.get_barrier_semaphore()
    for p, bits in every:
        pl.semaphore_signal(barrier, inc=1, device_id=device(p, bits), device_id_type=MESH)
    pl.semaphore_wait(barrier, len(every))

    copies = []
    for n, (p, bits) in enumerate(every):
        tz, tx, tc = target(p, bits)
        copies.append(
            pltpu.make_async_remote_copy(
                src_ref=send_ref.at[lax.rem(tz, 2) * 2 + tc, lax.rem(tx, 2), p],
                dst_ref=recv_ref.at[p, src, core],
                send_sem=send_sem.at[n],
                recv_sem=recv_sem.at[n],
                device_id=device(p, bits),
                device_id_type=MESH,
            )
        )
    n = len(every)
    copies.append(
        pltpu.make_async_remote_copy(
            src_ref=sens_ref,
            dst_ref=both_ref.at[core],
            send_sem=send_sem.at[n],
            recv_sem=recv_sem.at[n],
            device_id=(zh, zl, x, y, 1 - core),
            device_id_type=MESH,
        )
    )
    for copy in copies:
        copy.start()
    loads = [
        pltpu.make_async_copy(send_ref.at[zl * 2 + core, lax.rem(x, 2), p], keep.at[p], local_sem.at[p])
        for p in (0, 1)
    ] + [pltpu.make_async_copy(sens_ref, keep_sens, local_sem.at[2])]
    stores = [
        pltpu.make_async_copy(keep.at[p], recv_ref.at[p, src, core], local_sem.at[3 + p]) for p in (0, 1)
    ] + [pltpu.make_async_copy(keep_sens, both_ref.at[core], local_sem.at[5])]
    for load in loads:
        load.start()
    for load, store in zip(loads, stores):
        load.wait()
        store.start()
    for store in stores:
        store.wait()
    for copy in copies:
        copy.wait()


def exchange(slots, ident, send, sens):
    return pl.pallas_call(
        functools.partial(exchange_kernel, slots),
        in_specs=[pl.BlockSpec(memory_space=pl.ANY)] * 2,
        out_specs=[pl.BlockSpec(memory_space=pl.ANY)] * 2,
        out_shape=[
            jax.ShapeDtypeStruct((2, 4, 2, slots, 16, IMG), BF),
            jax.ShapeDtypeStruct((2, 4, IMG, IMG), BF),
        ],
        scratch_shapes=[
            pltpu.VMEM((2, slots, 16, IMG), BF),
            pltpu.VMEM((4, IMG, IMG), BF),
            pltpu.SemaphoreType.DMA((15,)),
            pltpu.SemaphoreType.DMA((15,)),
            pltpu.SemaphoreType.DMA((6,)),
        ],
        compiler_params=pltpu.CompilerParams(collective_id=ident, has_side_effects=True),
        name="exchange",
    )(send, sens)


YB = 64


def image_kernel(slots, meta_ref, data_ref, sens_ref, traj_ref, coef_ref, line_ref, basy_ref, basx_ref, out_ref, acc, sens, weights):
    total = meta_ref[0]
    acc[...] = jnp.zeros_like(acc)
    scale = 1.0 / (math.sqrt(128.0) * SHOTS)
    for s in range(2):
        for c in range(4):
            sens[s, :, c * YB:(c + 1) * YB, :] = (sens_ref[s, c].astype(F32) * scale).reshape(4, YB, IMG)
    lane = lax.broadcasted_iota(jnp.int32, (IMG, HALF), 1)
    coil = lax.rem(lane // 4, 4)
    masks = [coil == c for c in range(4)]
    kline = lax.broadcasted_iota(jnp.int32, (2 * IMG, HALF), 0)

    def unit(j, carry):
        code = meta_ref[1 + j]
        p = lax.rem(j, 2)
        slot = j // 2
        direction = code // SHOTS
        pick = (kline == traj_ref[code * 2 + p]).astype(F32).astype(BF)
        table = jnp.dot(line_ref[...], pick, preferred_element_type=F32)
        for c in range(4):
            weights[:, c * YB:(c + 1) * YB, :] = jnp.where(masks[c], table, 0.0).astype(BF).reshape(4, YB, HALF)
        coefs = coef_ref[code]
        mixed = jnp.dot(coefs, basx_ref[...], preferred_element_type=F32, precision=lax.Precision.HIGHEST)
        one = mixed.astype(BF)
        rest = mixed - one.astype(F32)
        two = rest.astype(BF)
        three = (rest - two.astype(F32)).astype(BF)
        mixed6 = jnp.concatenate([one, two, one, two, three, one], 0)
        rhs = []
        for s in range(2):
            rows = jnp.concatenate([data_ref[p, w, s, slot] for w in range(4)], 0)
            swapped = jnp.concatenate([-rows[:, HALF:], rows[:, :HALF]], 1)
            rhs.append(jnp.concatenate([rows, swapped], 0))

        for b in range(IMG // YB):
            turns = jnp.dot(basy_ref[b * YB:(b + 1) * YB, :], mixed6, preferred_element_type=F32)
            sine, cosine = sincos_turns(turns)
            ure = jnp.zeros((YB, HALF), F32)
            uim = jnp.zeros((YB, HALF), F32)
            for s in range(2):
                image = jnp.dot(weights[b], rhs[s], preferred_element_type=F32)
                for c in range(4):
                    ire, iim = image[c * YB:(c + 1) * YB, :HALF], image[c * YB:(c + 1) * YB, HALF:]
                    sre = sens[s, b, c * YB:(c + 1) * YB, :HALF]
                    sim = sens[s, b, c * YB:(c + 1) * YB, HALF:]
                    ure = ure + (sre * ire + sim * iim)
                    uim = uim + (sre * iim - sim * ire)
            acc[b, direction, :, :HALF] += cosine * ure + sine * uim
            acc[b, direction, :, HALF:] += cosine * uim - sine * ure
        return carry

    lax.fori_loop(0, total, unit, 0)
    out_ref[...] = acc[...].astype(BF)


def gridded(slots, meta, data, sens, traj, coefs, line, basy, basx):
    vm = pl.BlockSpec(memory_space=pltpu.VMEM)
    return pl.pallas_call(
        functools.partial(image_kernel, slots),
        in_specs=[pl.BlockSpec(memory_space=pltpu.SMEM)] + [vm] * 7,
        out_specs=vm,
        out_shape=jax.ShapeDtypeStruct((4, 16, YB, IMG), BF),
        scratch_shapes=[
            pltpu.VMEM((4, 16, YB, IMG), F32),
            pltpu.VMEM((2, 4, 4 * YB, IMG), F32),
            pltpu.VMEM((4, 4 * YB, HALF), BF),
        ],
        compiler_params=pltpu.CompilerParams(vmem_limit_bytes=48 << 20),
        cost_estimate=pl.CostEstimate(flops=2 * slots * 2048 * 256 * 256, bytes_accessed=16 << 20, transcendentals=0),
        name="gridded",
    )(meta, data, sens, traj, coefs, line, basy, basx)


def on_device(kspace, accept, trajectory, phase_coef, sens):
    zh, zl = lax.axis_index("zh"), lax.axis_index("zl")
    x, core = lax.axis_index("x"), lax.axis_index("core")
    half = lax.rem(x, 2)

    kept = accept.reshape(4, 2, 4, 2, SHOTS).transpose(1, 3, 0, 2, 4).reshape(4, 128)
    order = jnp.argsort(1 - kept, axis=1, stable=True)[:, :96]
    counts = jnp.sum(kept, axis=1)
    dir16, shot = order // SHOTS, order % SHOTS
    subset = jnp.arange(4)[:, None]
    direction = (dir16 // 4) * 16 + (subset // 2) * 8 + (dir16 % 4) * 2 + subset % 2
    source = direction * SHOTS + shot
    mine = zl * 2 + core
    meta = jnp.concatenate([lax.dynamic_slice_in_dim(counts, mine, 1, 0), lax.dynamic_index_in_dim(order, mine, 0, False)])

    small = jnp.concatenate(
        [
            lax.dynamic_index_in_dim(trajectory, core, 0, True).astype(F32),
            lax.dynamic_index_in_dim(phase_coef, core, 0, True).reshape(1, SHOTS, PB * PB),
        ],
        2,
    )
    small = lax.all_gather(small, ("zh", "x"), axis=0, tiled=True).reshape(128, 128 + PB * PB)
    coefs = small[:, 128:].reshape(128, PB, PB)
    k = jnp.arange(128)
    part, w, row = k // 64, (k // 16) % 4, k % 4
    wx, wz = w // 2, w % 2
    z = zh * 2 + zl
    picks = []
    for p in range(2):
        rx = jnp.where(wx == x % 2, x, partner(p, x, 4))
        rz = jnp.where(wz == z % 2, z, partner(p, z, 8))
        picks.append((rz * 4 + rx) * 4 + row)
    lines = jnp.concatenate(picks)
    choose = (jnp.arange(128)[:, None] == lines[None, :]).astype(BF)
    traj = jnp.dot(small[:, :128].astype(BF), choose, preferred_element_type=F32).astype(jnp.int32)
    traj = (traj.reshape(128, 2, 128) + IMG * part[None, None, :]).reshape(256, 1, 128)

    basis = basis_const()
    b1, b2, b3 = split3(basis / (2.0 * math.pi))
    basy = jnp.asarray(np.concatenate([b1, b1, b2, b2, b1, b3], 1))
    basx = lax.dynamic_slice_in_dim(jnp.asarray(basis.T.astype(np.float32)), half * HALF, HALF, 1)
    sens_half = jnp.concatenate(
        [
            lax.dynamic_slice_in_dim(sens, half * HALF, HALF, 2),
            lax.dynamic_slice_in_dim(sens, IMG + half * HALF, HALF, 2),
        ],
        2,
    )
    tab, line = readout_const(), line_const()
    flat = kspace.reshape(DIRS * SHOTS, 16, 2 * IMG)

    def run(ident, slots):
        def branch(flat, source, meta, sens_half, traj, coefs, basx):
            index = source[:, : 2 * slots].reshape(4, slots, 2).transpose(0, 2, 1).reshape(-1)
            send = readout(slots, flat, index, tab)
            data, both = exchange(slots, ident, send, sens_half)
            return gridded(slots, meta, data, both, traj, coefs, line, basy, basx)

        return branch

    need = jnp.max(counts)
    level = sum((need > 2 * s).astype(jnp.int32) for s in LEVELS[:-1])
    part_image = lax.switch(level, [run(i, s) for i, s in enumerate(LEVELS)], flat, source, meta, sens_half, traj, coefs, basx)

    rows = lax.all_to_all(part_image, "y", split_axis=0, concat_axis=0, tiled=True)
    rows = jnp.sum(rows.astype(F32), 0).astype(BF)
    rows = rows.reshape(16, 2, 32, IMG).reshape(32, 32, IMG)
    pieces = lax.all_to_all(rows, ("zh", "x", "core"), split_axis=0, concat_axis=0, tiled=True)
    pieces = pieces.reshape(4, 2, 2, 2, 32, 2, HALF).astype(F32)
    total = jnp.sum(pieces, axis=(0, 1))
    return total.transpose(1, 2, 3, 0, 4).reshape(2, 32, 2 * IMG)


def solution(mesh):
    inner = Mesh(mesh.devices.reshape(4, 2, 4, 4, 2), AXES)
    return jax.shard_map(
        on_device,
        mesh=inner,
        in_specs=(
            P(None, None, ("y", "core"), ("zh", "zl", "x"), None),
            P(),
            P(("zh", "zl", "x"), None, None),
            P(("zh", "zl", "x"), None, None, None),
            P(("y", "core"), None, None),
        ),
        out_specs=P(("zh", "zl", "x"), ("y", "core"), None),
        check_vma=False,
    )
```

time: 328 us -> 242 us (0.74)
  the two profiles are of different devices: /device:TPU:1 before, /device:TPU:33 now
where the time goes in v1:
time: 242 us; the launch traced here: 240 us
  Pallas kernels  106 us (44%)
  blocking collectives  91.4 us (38%)
  local copies, waits for them, and re-layouts  22.7 us (9%)
  between operations  15.5 us (6%)
  other arithmetic  4.05 us (2%)
    pallas_call x1, Pallas kernels, gridded(): pl.pallas_call(functools.partial(image_kernel, slots), in_specs=[pl.Block...  54.8 us
    all_gather x1, blocking collectives, on_device(): lax.all_gather(small, ('zh', 'x'), axis=0, tiled=True)  39.3 us
    pallas_call x1, Pallas kernels, exchange(): pl.pallas_call(functools.partial(exchange_kernel, slots), in_specs=[pl.Bl...  37.6 us
    all_to_all x1, blocking collectives, on_device(): lax.all_to_all(part_image, 'y', split_axis=0, concat_axis=0, tiled=True)  29.6 us
    all_to_all x1, blocking collectives, on_device(): lax.all_to_all(rows, ('zh', 'x', 'core'), split_axis=0, concat_axis=0, ti...  22.5 us
    pallas_call x1, Pallas kernels, readout(): pl.pallas_call(functools.partial(readout_kernel, count), grid_spec=pltpu....  13.7 us
    reshape x1, local copies, waits for them, and re-layouts, on_device(): flat = kspace.reshape(DIRS * SHOTS, 16, 2 * IMG)  12.6 us

profile of v1, /device:TPU:33, one launch (start us, length us, event | category | flops | bytes accessed | tf_op | source)
XLA Modules:
  0.0 240.2 jit_solution(12759959318813204518)
XLA Ops:
  6.5 0.0 copy-start
  6.5 0.0 sort.19.cloned.1.call-start
  6.5 0.8 copy.93
  7.3 0.2 bitcast_subtract_fusion
  7.5 0.7 sub.49
  8.2 0.6 iota.34
  8.8 0.0 sort.19.cloned.1.call-update
  8.9 0.7 dynamic-slice_convert_fusion
  9.6 0.0 copy-done
  9.6 0.1 reshape.147
  9.7 39.3 %all_gather.3 = f32[16,8,384]{2,1,0:T(8,128)S(1)} all-gather(f32[1,8,384]{2,1,0:T(8,128)S(1)} %pad_maximum_fusion.1), channel_id=1, replica_groups=mesh['zh'=4,'zl'=2,'x'=4,'y'=4,'core'=2] {'zh','x'}, dimensions={0}, use_global_device_ids=true | all-gather | bytes 208896 | tf_op jit(solution)/shard_map/all_gather | solution.py:299
  49.0 0.2 convolution_convert_fusion
  49.2 0.7 constant_dynamic-slice_fusion
  49.9 0.1 broadcast_add_fusion
  50.0 1.1 constant_dynamic-slice_fusion.4
  51.1 0.1 pad_maximum_fusion
  51.2 0.1 reduce_sum.33
  51.3 0.7 reduce_max.9
  53.9 0.1 copy.96
  54.0 0.0 copy-start.6
  54.0 0.0 copy-start.8
  54.0 12.6 %reshape.146 = bf16[512,16,512]{2,1,0:T(8,128)(2,1)} reshape(bf16[64,8,4,4,512]{4,3,2,1,0:T(4,128)(2,1)} %param.13) | data formatting | bytes 16777216 | tf_op jit(solution)/shard_map/reshape | solution.py:327
  66.6 0.6 dynamic_slice.26
  67.2 0.0 sort.19.cloned.1.call-done
  67.2 0.7 fusion.19
  68.0 0.6 pad_add_fusion.1
  68.6 0.0 copy-done.6
  68.6 0.0 copy-done.8
  68.6 109.0 %conditional.1 = (bf16[4,16,64,256]{3,2,1,0:T(8,128)(2,1)S(1)}) conditional(s32[]{:T(128)} %clamp.3, (s32[4,96]{1,0:T(4,128)S(1)}, bf16[512,512]{1,0:T(8,128)(2,1)S(1)}, bf16[512,16,512]{2,1,0:T(8,128)(2,1)}, bf16[4,256,256]{2,1,0:T(8,128)(2,1)S(1)}, s32[97]{0:T(128)S(1)}, /*index=5*/s32[256,1,128]{2,1,0:T(1,128)S(1)}, ...), branch_computations={%region_3.4_spmd, %region_4.5_spmd, %region_5.6_spmd, %region_6.7_... | conditional | flops 16106127360 | bytes 33825828 | solution.py:340
  68.6 0.1 copy.99
  68.7 0.1 copy.90
  68.8 0.7 reshape.133.idx_ref
  69.5 13.7 %readout.5.send_ref = bf16[4,2,2,36,16,256]{5,4,3,2,1,0:T(8,128)(2,1)} custom-call(s32[288]{0:T(512)} %reshape.133.idx_ref, bf16[512,512]{1,0:T(8,128)(2,1)S(1)} %get-tuple-element.104.tab_ref, ...), custom_call_target="tpu_custom_call" | custom-call | flops 2415919104 | bytes 9437184 | tf_op jit(solution)/shard_map/cond/branch_1_fun/readout/pallas_call | solution.py:92
  83.2 37.6 %exchange.5 = (bf16[2,4,2,36,16,256]{5,4,3,2,1,0:T(8,128)(2,1)}, bf16[2,4,256,256]{3,2,1,0:T(8,128)(2,1)}) custom-call(bf16[4,2,2,36,16,256]{5,4,3,2,1,0:T(8,128)(2,1)} %readout.5.send_ref, bf16[4,256,256]{2,1,0:T(8,128)(2,1)S(1)} %get-tuple-element.106.sens_ref), custom_call_target="tpu_custom_call" | custom-call | tf_op jit(solution)/shard_map/cond/branch_1_fun/exchange/pallas_call | solution.py:181
  120.9 0.5 copy.100.coef_ref
  121.3 0.0 copy-start.3
  121.4 1.2 copy-done.3
  122.6 54.8 %gridded.5 = bf16[4,16,64,256]{3,2,1,0:T(8,128)(2,1)S(1)} custom-call(s32[97]{0:T(128)S(1)} %get-tuple-element.102.meta_ref, bf16[2,4,2,36,16,256]{5,4,3,2,1,0:T(8,128)(2,1)} %get-tuple-element.107.data_ref, bf16[2,4,256,256]{3,2,1,0:T(8,128)(2,1)S(1)} %copy-done.3, s32[256,1,128]{2,1,0:T(1,128)S(1)} %get-tuple-element.109.traj_ref, ...), custom_call_target="tpu_custom_call" | custom-call | flops 9663676416 | bytes 16777216 | tf_op jit(solution)/shard_map/cond/branch_1_fun/gridded/pallas_call | solution.py:261
  177.6 0.0 copy-start.7
  177.6 1.3 copy-done.7
  178.9 0.0 copy-start.1
  178.9 29.6 %all_to_all.10 = bf16[4,16,64,256]{3,2,1,0:T(8,128)(2,1)S(1)} all-to-all(bf16[4,16,64,256]{3,2,1,0:T(8,128)(2,1)} %copy-done.7), channel_id=1, replica_groups=mesh['zh'=4,'zl'=2,'x'=4,'y'=4,'core'=2] {'y'}, dimensions={0} | all-to-all | bytes 4194304 | tf_op jit(solution)/shard_map/all_to_all | solution.py:342
  208.5 0.4 reduce_sum.34
  208.9 22.5 %all_to_all.11 = bf16[32,32,256]{2,1,0:T(8,128)(2,1)S(1)} all-to-all(bf16[32,32,256]{2,1,0:T(8,128)(2,1)S(1)} %bitcast.31), channel_id=1, replica_groups=mesh['zh'=4,'zl'=2,'x'=4,'y'=4,'core'=2] {'zh','x','core'}, dimensions={0} | all-to-all | bytes 1048576 | tf_op jit(solution)/shard_map/all_to_all | solution.py:345
  231.4 0.5 reshape.152
  231.9 0.5 reduce_sum.35
  232.4 0.1 copy.106
  232.6 0.8 reshape.151
  233.3 0.0 copy-done.1
  (11 shorter events, 0.1 us)
Async XLA Ops:
  6.5 3.0 %copy-start = (f32[2,8,16,16]{3,2,1,0:T(8,128)S(1)}, f32[2,8,16,16]{3,2,1,0:T(8,128)}, u32[]{:S(2)}) copy-start(f32[2,8,16,16]{3,2,1,0:T(8,128)} %param.16) | copy-start | bytes 49156
  6.5 60.7 %sort.19.cloned.1.call-start = ((), (), s32[]{:S(2)}) async-start(), calls=%async_computation.2 | async-start | bytes 12320 | tf_op jit(solution)/shard_map/jit(argsort)/sort | solution.py:283
  54.0 14.6 %copy-start.6 = (bf16[512,512]{1,0:T(8,128)(2,1)S(1)}, bf16[512,512]{1,0:T(8,128)(2,1)}, u32[]{:S(2)}) copy-start(bf16[512,512]{1,0:T(8,128)(2,1)} %constant.226) | copy-start | bytes 1572868
  54.0 14.6 %copy-start.8 = (bf16[256,96]{1,0:T(8,128)(2,1)S(1)}, bf16[256,96]{1,0:T(8,128)(2,1)}, u32[]{:S(2)}) copy-start(bf16[256,96]{1,0:T(8,128)(2,1)} %constant.218.clone) | copy-start | bytes 147460
  121.3 1.2 copy-start.3
  177.6 1.3 copy-start.7
  178.9 54.4 %copy-start.1 = (f32[2,8,16,16]{3,2,1,0:T(8,128)S(1)}, f32[2,8,16,16]{3,2,1,0:T(8,128)}, u32[]{:S(2)}) copy-start(f32[2,8,16,16]{3,2,1,0:T(8,128)} %param.16) | copy-start | bytes 49156
Sparse Core Ops, SparseCore 0:
  9.6 2.0 sort.21.cloned.1.call-done
  (1 shorter events, 0.0 us)

commit v2 on v1

v2 whole, which is shorter than its diff:
```python
import functools
import math

import jax
import jax.numpy as jnp
import numpy as np
from jax import lax
from jax.experimental import pallas as pl
from jax.experimental.pallas import tpu as pltpu
from jax.sharding import Mesh, PartitionSpec as P

IMG = 256
SHOTS = 8
PB = 16
DIRS = 64
HALF = IMG // 2
MESH = pl.DeviceIdType.MESH
AXES = ("zh", "zl", "x", "y", "core")
BF = jnp.bfloat16
F32 = jnp.float32

LEVELS = (32, 36, 48)
STEP = {32: 16, 36: 18, 48: 16}


def readout_const():
    k = np.arange(IMG)
    ang = (np.outer(k, k) % IMG).astype(np.float64) * (2.0 * np.pi / IMG)
    c, s = np.cos(ang).astype(np.float32), np.sin(ang).astype(np.float32)
    tab = np.concatenate([np.concatenate([c, s], 1), np.concatenate([-s, c], 1)], 0)
    order = np.concatenate([np.arange(HALF), IMG + np.arange(HALF), HALF + np.arange(HALF), IMG + HALF + np.arange(HALF)])
    return jnp.asarray(tab[:, order]).astype(BF)


def line_const():
    k = np.arange(IMG)
    ang = (np.outer(k, k) % IMG).astype(np.float64) * (2.0 * np.pi / IMG)
    return jnp.asarray(np.concatenate([np.cos(ang), np.sin(ang)], 1).astype(np.float32)).astype(BF)


def basis_const():
    points = np.arange(IMG, dtype=np.float64)
    orders = np.arange(PB, dtype=np.float64)
    return np.cos(np.pi * orders[None, :] * (points[:, None] + 0.5) / IMG)


def split3(a):
    one = np.asarray(a, np.float32).astype(BF)
    rest = np.asarray(a, np.float64) - one.astype(np.float64)
    two = rest.astype(np.float32).astype(BF)
    rest = rest - two.astype(np.float64)
    return one, two, rest.astype(np.float32).astype(BF)


def poly_consts():
    u = np.cos(np.linspace(0, np.pi, 4001)) * 0.125 + 0.125
    t = np.sqrt(np.maximum(u, 0))
    fs = np.where(t > 1e-9, np.sin(2 * np.pi * t) / np.where(t > 1e-9, t, 1), 2 * np.pi)
    return [float(v) for v in np.polyfit(u, fs, 5)], [float(v) for v in np.polyfit(u, np.cos(2 * np.pi * t), 6)]


SIN_C, COS_C = poly_consts()


def sincos_turns(turns):
    t = turns - jnp.round(turns)
    u = t * t
    s = jnp.full_like(u, SIN_C[0])
    for v in SIN_C[1:]:
        s = s * u + v
    c = jnp.full_like(u, COS_C[0])
    for v in COS_C[1:]:
        c = c * u + v
    return s * t, c


def partner(p, i, n):
    if p == 0:
        return i + 1 - 2 * lax.rem(i, 2)
    return lax.rem(i + 2 * lax.rem(i, 2) - 1 + n, n)


def exchange_kernel(slots, idx_ref, tab_ref, small_ref, kspace_ref, sens_ref, recv_ref, both_ref, gath_ref,
                    kv, send, keep_sens, load_sem, send_sem, recv_sem, local_sem):
    zh, zl = lax.axis_index("zh"), lax.axis_index("zl")
    x, y, core = lax.axis_index("x"), lax.axis_index("y"), lax.axis_index("core")
    z = zh * 2 + zl
    half = lax.rem(x, 2)
    src = half * 2 + zl
    count = STEP[slots]

    load = pltpu.make_async_copy(kspace_ref, kv, load_sem)
    load.start()
    load_sens = pltpu.make_async_copy(sens_ref, keep_sens, local_sem.at[2])
    load_sens.start()

    def target(p, bits):
        bx, bz, bc = bits
        tx = partner(p, x, 4) if bx else x
        tz = partner(p, z, 8) if bz else z
        tc = 1 - core if bc else core
        return tz, tx, tc

    def device(p, bits):
        tz, tx, tc = target(p, bits)
        return (tz // 2, lax.rem(tz, 2), tx, y, tc)

    groups = [(bz, bc, p) for bz in (1, 0) for bc in (0, 1) for p in (0, 1)]
    every = [(p, (bx, bz, bc)) for bz, bc, p in groups for bx in (1, 0) if bx + bz + bc]
    spread = [(dz, dx) for dz in range(4) for dx in range(4) if dz + dx]

    def far(shift):
        return (lax.rem(zh + shift[0], 4), zl, lax.rem(x + shift[1], 4), y, core)

    barrier = pltpu.get_barrier_semaphore()
    for p, bits in every:
        pl.semaphore_signal(barrier, inc=1, device_id=device(p, bits), device_id_type=MESH)
    for shift in spread:
        pl.semaphore_signal(barrier, inc=1, device_id=far(shift), device_id_type=MESH)
    pl.semaphore_wait(barrier, len(every) + len(spread))

    copies = []
    n_every = len(every)

    def begin(src_ref, dst_ref, n, where):
        copy = pltpu.make_async_remote_copy(
            src_ref=src_ref, dst_ref=dst_ref, send_sem=send_sem.at[n], recv_sem=recv_sem.at[n],
            device_id=where, device_id_type=MESH,
        )
        copy.start()
        copies.append(copy)

    for n, shift in enumerate(spread):
        begin(small_ref, gath_ref.at[zh * 4 + x], n_every + 1 + n, far(shift))
    locals_ = [pltpu.make_async_copy(small_ref, gath_ref.at[zh * 4 + x], local_sem.at[3])]
    locals_[0].start()
    load_sens.wait()
    begin(keep_sens, both_ref.at[core], n_every, (zh, zl, x, y, 1 - core))
    store = pltpu.make_async_copy(keep_sens, both_ref.at[core], local_sem.at[2])
    store.start()
    locals_.append(store)
    load.wait()

    for g, (bz, bc, p) in enumerate(groups):
        tz, _, tc = target(p, (0, bz, bc))
        base = ((lax.rem(tz, 2) * 2 + tc) * 2 + p) * slots

        def transform(b, carry):
            rows = jnp.concatenate(
                [kv[idx_ref[base + b * count + i]].reshape(16, 2 * IMG) for i in range(count)], 0
            )
            spec = jnp.dot(rows, tab_ref[...], preferred_element_type=F32) * (1.0 / math.sqrt(IMG))
            spec = spec.astype(BF).reshape(count, 16, 2 * IMG)
            send[g, 0, pl.ds(b * count, count)] = spec[:, :, :IMG]
            send[g, 1, pl.ds(b * count, count)] = spec[:, :, IMG:]
            return carry

        lax.fori_loop(0, slots // count, transform, 0)
        for bx in (1, 0):
            column = 1 - half if bx else half
            if bx + bz + bc:
                begin(send.at[g, column], recv_ref.at[p, src, core], every.index((p, (bx, bz, bc))), device(p, (bx, bz, bc)))
            else:
                copy = pltpu.make_async_copy(send.at[g, column], recv_ref.at[p, src, core], local_sem.at[p])
                copy.start()
                locals_.append(copy)
    for copy in locals_:
        copy.wait()
    for copy in copies:
        copy.wait()


def exchange(slots, ident, index, tab, small, kspace, sens):
    any_ = pl.BlockSpec(memory_space=pl.ANY)
    vm = pl.BlockSpec(memory_space=pltpu.VMEM)
    return pl.pallas_call(
        functools.partial(exchange_kernel, slots),
        in_specs=[pl.BlockSpec(memory_space=pltpu.SMEM), vm, vm, any_, any_],
        out_specs=[any_] * 3,
        out_shape=[
            jax.ShapeDtypeStruct((2, 4, 2, slots, 16, IMG), BF),
            jax.ShapeDtypeStruct((2, 4, IMG, IMG), BF),
            jax.ShapeDtypeStruct((16, 24, 128), F32),
        ],
        scratch_shapes=[
            pltpu.VMEM((DIRS * SHOTS, 4, 4, 2 * IMG), BF),
            pltpu.VMEM((8, 2, slots, 16, IMG), BF),
            pltpu.VMEM((4, IMG, IMG), BF),
            pltpu.SemaphoreType.DMA,
            pltpu.SemaphoreType.DMA((30,)),
            pltpu.SemaphoreType.DMA((30,)),
            pltpu.SemaphoreType.DMA((4,)),
        ],
        compiler_params=pltpu.CompilerParams(collective_id=ident, has_side_effects=True, vmem_limit_bytes=40 << 20),
        cost_estimate=pl.CostEstimate(flops=8 * slots * 16 * 512 * 512 * 2, bytes_accessed=16 << 20, transcendentals=0),
        name="exchange",
    )(index, tab, small, kspace, sens)


YB = 64


def image_kernel(slots, meta_ref, data_ref, sens_ref, gath_ref, choose_ref, line_ref, basy_ref, basx_ref, out_ref,
                 acc, sens, weights_a, weights_b, traj, mixes):
    total = meta_ref[0]
    acc[...] = jnp.zeros_like(acc)
    scale = 1.0 / (math.sqrt(128.0) * SHOTS)
    for s in range(2):
        for c in range(4):
            sens[s, :, c * YB:(c + 1) * YB, :] = (sens_ref[s, c].astype(F32) * scale).reshape(4, YB, IMG)

    lines = jnp.dot(gath_ref[:, :8, :].reshape(128, 128).astype(BF), choose_ref[...], preferred_element_type=F32)
    traj[0] = lines[:, :128]
    traj[1] = lines[:, 128:]

    flat = gath_ref[:, 8:, :].reshape(256, 128)
    one = flat.astype(BF)
    rest = flat - one.astype(F32)
    two = rest.astype(BF)
    three = (rest - two.astype(F32)).astype(BF)
    flat6 = jnp.concatenate([one, one, two, two, one, three], 1)
    shot_row = lax.broadcasted_iota(jnp.int32, (128, 128), 0) // PB
    for s in range(SHOTS):
        b1, b2, b3 = [jnp.where(shot_row == s, basx_ref[i].astype(F32), 0.0).astype(BF) for i in range(3)]
        mixes[s] = jnp.dot(flat6, jnp.concatenate([b1, b2, b1, b2, b3, b1], 0), preferred_element_type=F32)

    lane = lax.broadcasted_iota(jnp.int32, (1, HALF), 1)
    coil = lax.rem(lane // 4, 4)
    masks = [jnp.where(coil == c, 1.0, 0.0).astype(BF) for c in range(4)]
    first = lane < 64
    kline = lax.broadcasted_iota(jnp.int32, (IMG, HALF), 0).astype(F32)

    def prepare(j, p, weights):
        code = meta_ref[1 + j]
        pick = jnp.where(kline == traj[p, pl.ds(code, 1), :], 1.0, 0.0).astype(BF)
        cosine = jnp.dot(line_ref[0], pick, preferred_element_type=F32)
        sine = jnp.dot(line_ref[1], pick, preferred_element_type=F32)
        table = jnp.where(first, cosine, sine).astype(BF)
        for c in range(4):
            weights[:, c * YB:(c + 1) * YB, :] = (table * masks[c]).reshape(4, YB, HALF)

    def combine(j, p, slot, weights):
        code = meta_ref[1 + j]
        direction = jnp.where(j < total, code // SHOTS, 16)
        mixed = mixes[lax.rem(code, SHOTS), pl.ds(pl.multiple_of((code // SHOTS) * PB, PB), PB), :]
        one = mixed.astype(BF)
        rest = mixed - one.astype(F32)
        two = rest.astype(BF)
        three = (rest - two.astype(F32)).astype(BF)
        mixed6 = jnp.concatenate([one, two, one, two, three, one], 0)
        rhs = []
        for s in range(2):
            rows = jnp.concatenate([data_ref[p, w, s, slot] for w in range(4)], 0)
            swapped = jnp.concatenate([-rows[:, HALF:], rows[:, :HALF]], 1)
            rhs.append(jnp.concatenate([rows, swapped], 0))
        for b in range(IMG // YB):
            turns = jnp.dot(basy_ref[b * YB:(b + 1) * YB, :], mixed6, preferred_element_type=F32)
            sine, cosine = sincos_turns(turns)
            ure = uim = None
            for s in range(2):
                image = jnp.dot(weights[b], rhs[s], preferred_element_type=F32)
                for c in range(4):
                    ire, iim = image[c * YB:(c + 1) * YB, :HALF], image[c * YB:(c + 1) * YB, HALF:]
                    sre = sens[s, b, c * YB:(c + 1) * YB, :HALF]
                    sim = sens[s, b, c * YB:(c + 1) * YB, HALF:]
                    re = sre * ire + sim * iim
                    im = sre * iim - sim * ire
                    ure = re if ure is None else ure + re
                    uim = im if uim is None else uim + im
            acc[b, direction, :, :HALF] += cosine * ure + sine * uim
            acc[b, direction, :, HALF:] += cosine * uim - sine * ure

    prepare(0, 0, weights_a)

    def pair(i, carry):
        prepare(2 * i + 1, 1, weights_b)
        combine(2 * i, 0, i, weights_a)
        prepare(2 * i + 2, 0, weights_a)
        combine(2 * i + 1, 1, i, weights_b)
        return carry

    lax.fori_loop(0, (total + 1) // 2, pair, 0)
    out_ref[...] = acc[:, :16].astype(BF)


def gridded(slots, meta, data, sens, gath, choose, line, basy, basx):
    vm = pl.BlockSpec(memory_space=pltpu.VMEM)
    return pl.pallas_call(
        functools.partial(image_kernel, slots),
        in_specs=[pl.BlockSpec(memory_space=pltpu.SMEM)] + [vm] * 7,
        out_specs=vm,
        out_shape=jax.ShapeDtypeStruct((4, 16, YB, IMG), BF),
        scratch_shapes=[
            pltpu.VMEM((4, 17, YB, IMG), F32),
            pltpu.VMEM((2, 4, 4 * YB, IMG), F32),
            pltpu.VMEM((4, 4 * YB, HALF), BF),
            pltpu.VMEM((4, 4 * YB, HALF), BF),
            pltpu.VMEM((2, 128, 128), F32),
            pltpu.VMEM((SHOTS, 256, 128), F32),
        ],
        compiler_params=pltpu.CompilerParams(vmem_limit_bytes=48 << 20),
        cost_estimate=pl.CostEstimate(flops=2 * slots * 2048 * 256 * 256, bytes_accessed=16 << 20, transcendentals=0),
        name="gridded",
    )(meta, data, sens, gath, choose, line, basy, basx)


def on_device(kspace, accept, trajectory, phase_coef, sens):
    zh, zl = lax.axis_index("zh"), lax.axis_index("zl")
    x, core = lax.axis_index("x"), lax.axis_index("core")
    half = lax.rem(x, 2)

    kept = accept.reshape(4, 2, 4, 2, SHOTS).transpose(1, 3, 0, 2, 4).reshape(4, 128)
    upto = np.triu(np.ones((128, 128), np.float32))
    place = jnp.dot(kept.astype(F32), jnp.asarray(upto), preferred_element_type=F32).astype(jnp.int32) - 1
    place = jnp.where(kept > 0, place, -1)
    unit = jnp.arange(128, dtype=jnp.int32)
    order = jnp.sum(jnp.where(place[:, None, :] == jnp.arange(96)[None, :, None], unit[None, None, :], 0), 2)
    counts = jnp.sum(kept, axis=1)
    dir16, shot = order // SHOTS, order % SHOTS
    subset = jnp.arange(4)[:, None]
    direction = (dir16 // 4) * 16 + (subset // 2) * 8 + (dir16 % 4) * 2 + subset % 2
    source = direction * SHOTS + shot
    mine = zl * 2 + core
    meta = jnp.concatenate(
        [
            lax.dynamic_slice_in_dim(counts, mine, 1, 0),
            lax.dynamic_index_in_dim(order, mine, 0, False),
            jnp.zeros((7,), jnp.int32),
        ]
    )

    small = jnp.concatenate(
        [
            lax.dynamic_index_in_dim(trajectory, core, 0, False).astype(F32),
            lax.dynamic_index_in_dim(phase_coef, core, 0, False).transpose(1, 0, 2).reshape(PB, SHOTS * PB),
        ],
        0,
    )
    k = jnp.arange(128)
    w, row = (k // 16) % 4, k % 4
    wx, wz = w // 2, w % 2
    z = zh * 2 + zl
    picks = []
    for p in range(2):
        rx = jnp.where(wx == x % 2, x, partner(p, x, 4))
        rz = jnp.where(wz == z % 2, z, partner(p, z, 8))
        picks.append((rz * 4 + rx) * 4 + row)
    choose = (jnp.arange(128)[:, None] == jnp.concatenate(picks)[None, :]).astype(BF)

    basis = basis_const()
    b1, b2, b3 = split3(basis / (2.0 * math.pi))
    basy = jnp.asarray(np.concatenate([b1, b1, b2, b2, b1, b3], 1))
    basx = jnp.asarray(np.stack([np.tile(np.asarray(part).T, (SHOTS, 1)) for part in split3(basis)]))
    basx = lax.dynamic_slice_in_dim(basx, half * HALF, HALF, 2)
    sens_half = jnp.concatenate(
        [
            lax.dynamic_slice_in_dim(sens, half * HALF, HALF, 2),
            lax.dynamic_slice_in_dim(sens, IMG + half * HALF, HALF, 2),
        ],
        2,
    )
    tab = readout_const()
    line = jnp.stack(jnp.split(line_const(), 2, 1))
    flat = kspace.reshape(DIRS * SHOTS, 4, 4, 2 * IMG)

    def run(ident, slots):
        def branch(flat, source, meta, sens_half, small, choose, basx):
            index = source[:, : 2 * slots].reshape(4, slots, 2).transpose(0, 2, 1).reshape(-1)
            data, both, gath = exchange(slots, ident, index, tab, small, flat, sens_half)
            return gridded(slots, meta, data, both, gath, choose, line, basy, basx)

        return branch

    need = jnp.max(counts)
    level = sum((need > 2 * s).astype(jnp.int32) for s in LEVELS[:-1])
    part_image = lax.switch(level, [run(i, s) for i, s in enumerate(LEVELS)], flat, source, meta, sens_half, small, choose, basx)

    rows = lax.all_to_all(part_image, "y", split_axis=0, concat_axis=0, tiled=True)
    rows = jnp.sum(rows.astype(F32), 0).astype(BF)
    rows = rows.reshape(16, 2, 32, IMG).reshape(32, 32, IMG)
    pieces = lax.all_to_all(rows, ("zh", "x", "core"), split_axis=0, concat_axis=0, tiled=True)
    pieces = pieces.reshape(4, 2, 2, 2, 32, 2, HALF).astype(F32)
    total = jnp.sum(pieces, axis=(0, 1))
    return total.transpose(1, 2, 3, 0, 4).reshape(2, 32, 2 * IMG)


def solution(mesh):
    inner = Mesh(mesh.devices.reshape(4, 2, 4, 4, 2), AXES)
    return jax.shard_map(
        on_device,
        mesh=inner,
        in_specs=(
            P(None, None, ("y", "core"), ("zh", "zl", "x"), None),
            P(),
            P(("zh", "zl", "x"), None, None),
            P(("zh", "zl", "x"), None, None, None),
            P(("y", "core"), None, None),
        ),
        out_specs=P(("zh", "zl", "x"), ("y", "core"), None),
        check_vma=False,
    )
```

time: 242 us -> 151 us (0.62)
  blocking collectives: 91.4 us -> 52.2 us
  Pallas kernels: 106 us -> 85.2 us
  local copies, waits for them, and re-layouts: 22.7 us -> 6.86 us
  between operations: 15.5 us -> 1.51 us
    all_gather x1 -> x0, blocking collectives: 39.3 us -> none  [on_device(): lax.all_gather(small, ('zh', 'x'), axis=0, tiled=True)]
    pallas_call x1 -> x0, Pallas kernels: 13.7 us -> none  [readout(): pl.pallas_call(functools.partial(readout_kernel, count), grid_spec=pltpu....]
    reshape x3 -> x1, local copies, waits for them, and re-layouts: 12.7 us -> 0.08 us  [on_device(): lax.dynamic_index_in_dim(phase_coef, core, 0, False).transpose(1, 0, 2)]
    pallas_call x1, Pallas kernels: 54.8 us -> 44 us  [gridded(): pl.pallas_call(functools.partial(image_kernel, slots), in_specs=[pl.Block...]
    pallas_call x1, Pallas kernels: 37.6 us -> 41.3 us  [exchange(): pl.pallas_call(functools.partial(exchange_kernel, slots), in_specs=[pl.Bl...]
where the time goes in v2:
time: 151 us; the launch traced here: 150 us
  Pallas kernels  85.2 us (56%)
  blocking collectives  52.2 us (35%)
  local copies, waits for them, and re-layouts  6.86 us (5%)
  other arithmetic  3.48 us (2%)
  between operations  1.51 us (1%)
    pallas_call x1, Pallas kernels, gridded(): pl.pallas_call(functools.partial(image_kernel, slots), in_specs=[pl.Block...  44 us
    pallas_call x1, Pallas kernels, exchange(): pl.pallas_call(functools.partial(exchange_kernel, slots), in_specs=[pl.Bl...  41.3 us
    all_to_all x1, blocking collectives, on_device(): lax.all_to_all(part_image, 'y', split_axis=0, concat_axis=0, tiled=True)  29.7 us
    all_to_all x1, blocking collectives, on_device(): lax.all_to_all(rows, ('zh', 'x', 'core'), split_axis=0, concat_axis=0, ti...  22.5 us

profile of v2, /device:TPU:33, one launch (start us, length us, event | category | flops | bytes accessed | tf_op | source)
XLA Modules:
  0.0 150.4 jit_solution(16449074316512799365)
XLA Ops:
  0.0 0.0 copy-start
  0.0 0.0 copy-start.4
  0.0 0.0 copy-start.3
  0.0 0.0 copy-start.5
  0.1 0.8 copy.49
  0.9 0.2 bitcast_reduce_fusion
  1.1 0.1 reduce_sum.43
  1.2 0.6 reduce_max.9
  3.2 0.1 convert_element_type.41
  3.3 0.1 gt.19
  3.4 0.9 fusion.2
  4.3 0.1 select_reduce_fusion
  4.4 0.6 dynamic_slice.28
  5.1 0.7 convert_bitcast_fusion
  5.8 0.0 copy-done
  5.8 0.1 reshape.96
  5.9 0.1 fusion.9
  6.0 0.9 constant_dynamic-slice_fusion
  6.9 1.1 constant_dynamic-slice_fusion.3
  8.0 0.1 pad_maximum_fusion
  8.0 0.7 pad_add_fusion.1
  8.7 0.0 copy-done.4
  8.7 0.0 copy-done.3
  8.8 0.0 copy-done.5
  8.8 85.8 %conditional.1 = (bf16[4,16,64,256]{3,2,1,0:T(8,128)(2,1)S(1)}) conditional(s32[]{:T(128)} %clamp.3, (s32[4,96]{1,0:T(4,128)S(1)}, bf16[512,512]{1,0:T(8,128)(2,1)S(1)}, f32[24,128]{1,0:T(8,128)S(1)}, bf16[512,4,4,512]{3,2,1,0:T(4,128)(2,1)}, bf16[4,256,256]{2,1,0:T(8,128)(2,1)S(1)}, /*index=5*/s32[104]{0:T(128)S(1)}, ...), branch_computations={%region_3.4_spmd, %region_4.5_spmd, %region_5.6_spmd} | conditional | flops 16106127360 | bytes 58729508 | solution.py:376
  8.8 0.1 copy.53
  8.9 0.1 copy.47
  9.0 0.1 reshape.88.idx_ref
  9.1 41.3 %exchange.4 = (bf16[2,4,2,36,16,256]{5,4,3,2,1,0:T(8,128)(2,1)S(1)}, bf16[2,4,256,256]{3,2,1,0:T(8,128)(2,1)S(1)}, f32[16,24,128]{2,1,0:T(8,128)S(1)}) custom-call(s32[288]{0:T(512)S(1)} %reshape.88.idx_ref, bf16[512,512]{1,0:T(8,128)(2,1)S(1)} %get-tuple-element.84.tab_ref, f32[24,128]{1,0:T(8,128)S(1)} %get-tuple-element.85.small_ref, ...), custom_call_target="tpu_custom_call" | custom-call | flops 2415919104 | bytes 16777216 | tf_op jit(solution)/shard_map/cond/branch_1_fun/exchange/pallas_call | solution.py:176
  50.4 44.0 %gridded.4 = bf16[4,16,64,256]{3,2,1,0:T(8,128)(2,1)S(1)} custom-call(s32[104]{0:T(128)S(1)} %get-tuple-element.82.meta_ref, bf16[2,4,2,36,16,256]{5,4,3,2,1,0:T(8,128)(2,1)S(1)} %get-tuple-element.88.data_ref, bf16[2,4,256,256]{3,2,1,0:T(8,128)(2,1)S(1)} %get-tuple-element.89.sens_ref, f32[16,24,128]{2,1,0:T(8,128)S(1)} %get-tuple-element.90.gath_ref, ...), custom_call_target="tpu_custom_call" | custom-call | flops 9663676416 | bytes 16777216 | tf_op jit(solution)/shard_map/cond/branch_1_fun/gridded/pallas_call | solution.py:288
  94.5 0.0 copy-start.2
  94.6 1.3 copy-done.2
  95.9 29.7 %all_to_all.10 = bf16[4,16,64,256]{3,2,1,0:T(8,128)(2,1)S(1)} all-to-all(bf16[4,16,64,256]{3,2,1,0:T(8,128)(2,1)} %copy-done.2), channel_id=1, replica_groups=mesh['zh'=4,'zl'=2,'x'=4,'y'=4,'core'=2] {'y'}, dimensions={0} | all-to-all | bytes 4194304 | tf_op jit(solution)/shard_map/all_to_all | solution.py:378
  125.6 0.4 reduce_sum.44
  126.0 22.5 %all_to_all.11 = bf16[32,32,256]{2,1,0:T(8,128)(2,1)S(1)} all-to-all(bf16[32,32,256]{2,1,0:T(8,128)(2,1)S(1)} %bitcast.36), channel_id=1, replica_groups=mesh['zh'=4,'zl'=2,'x'=4,'y'=4,'core'=2] {'zh','x','core'}, dimensions={0} | all-to-all | bytes 1048576 | tf_op jit(solution)/shard_map/all_to_all | solution.py:381
  148.5 0.5 reshape.99
  149.0 0.5 reduce_sum.45
  149.5 0.1 copy.56
  149.6 0.8 reshape.98
  (13 shorter events, 0.1 us)
Async XLA Ops:
  0.0 5.8 %copy-start = (f32[2,8,16,16]{3,2,1,0:T(8,128)S(1)}, f32[2,8,16,16]{3,2,1,0:T(8,128)}, u32[]{:S(2)}) copy-start(f32[2,8,16,16]{3,2,1,0:T(8,128)} %param.16) | copy-start | bytes 49156
  0.0 8.7 %copy-start.4 = (bf16[2,256,256]{2,1,0:T(8,128)(2,1)S(1)}, bf16[2,256,256]{2,1,0:T(8,128)(2,1)}, u32[]{:S(2)}) copy-start(bf16[2,256,256]{2,1,0:T(8,128)(2,1)} %constant.223) | copy-start | bytes 786436
  0.0 8.7 %copy-start.3 = (bf16[512,512]{1,0:T(8,128)(2,1)S(1)}, bf16[512,512]{1,0:T(8,128)(2,1)}, u32[]{:S(2)}) copy-start(bf16[512,512]{1,0:T(8,128)(2,1)} %constant.217) | copy-start | bytes 1572868
  0.0 8.7 %copy-start.5 = (bf16[256,96]{1,0:T(8,128)(2,1)S(1)}, bf16[256,96]{1,0:T(8,128)(2,1)}, u32[]{:S(2)}) copy-start(bf16[256,96]{1,0:T(8,128)(2,1)} %constant.209.clone) | copy-start | bytes 147460
  94.5 1.3 copy-start.2

commit v3 on v2

--- a/solution.py
+++ b/solution.py
@@ -131,8 +131,8 @@
         copies.append(copy)
 
     for n, shift in enumerate(spread):
-        begin(small_ref, gath_ref.at[zh * 4 + x], n_every + 1 + n, far(shift))
-    locals_ = [pltpu.make_async_copy(small_ref, gath_ref.at[zh * 4 + x], local_sem.at[3])]
+        begin(small_ref, gath_ref.at[lax.rem(x - zh + 4, 4) * 4 + zh], n_every + 1 + n, far(shift))
+    locals_ = [pltpu.make_async_copy(small_ref, gath_ref.at[lax.rem(x - zh + 4, 4) * 4 + zh], local_sem.at[3])]
     locals_[0].start()
     load_sens.wait()
     begin(keep_sens, both_ref.at[core], n_every, (zh, zl, x, y, 1 - core))
@@ -304,12 +304,112 @@
     )(meta, data, sens, gath, choose, line, basy, basx)
 
 
+def reduce_kernel(part_ref, out_ref, yr, zs, zr, ysend, yrecv, zsend, zrecv):
+    zh, zl = lax.axis_index("zh"), lax.axis_index("zl")
+    x, y, core = lax.axis_index("x"), lax.axis_index("y"), lax.axis_index("core")
+
+    def along(r):
+        return (zh, zl, x, lax.rem(y + r, 4), core)
+
+    def away(dz, dx, dc):
+        return (lax.rem(zh + dz, 4), zl, lax.rem(x + dx, 4), y, 1 - core if dc else core)
+
+    shifts = [(dz, (dz + t) % 4, dc) for t in range(4) for dz in range(4) for dc in range(2)]
+    barrier = pltpu.get_barrier_semaphore()
+    for r in (1, 2, 3):
+        pl.semaphore_signal(barrier, inc=1, device_id=along(r), device_id_type=MESH)
+    for shift in shifts[1:]:
+        pl.semaphore_signal(barrier, inc=1, device_id=away(*shift), device_id_type=MESH)
+    pl.semaphore_wait(barrier, 34)
+
+    def group(t):
+        return lax.rem(x - zh + t + 4, 4)
+
+    rows = []
+    for t in range(4):
+        for r in (2, 1, 3):
+            copy = pltpu.make_async_remote_copy(
+                src_ref=part_ref.at[lax.rem(y + r, 4), pl.ds(group(t) * 4, 4)],
+                dst_ref=yr.at[t, r - 1],
+                send_sem=ysend.at[t, r - 1],
+                recv_sem=yrecv.at[t, r - 1],
+                device_id=along(r),
+                device_id_type=MESH,
+            )
+            copy.start()
+            rows.append(copy)
+    pieces = []
+    for t in range(4):
+        for copy in rows[3 * t:3 * t + 3]:
+            copy.wait_recv()
+        for dz in range(4):
+            there = lax.rem(zh + dz, 4)
+            total = part_ref[y, group(t) * 4 + there].astype(F32)
+            for r in range(3):
+                total = total + yr[t, r, there].astype(F32)
+            for dc in range(2):
+                n = (t * 4 + dz) * 2 + dc
+                zs[n * 2:n * 2 + 2] = total.astype(BF).reshape(2, 32, IMG)
+                to = 1 - core if dc else core
+                if n:
+                    copy = pltpu.make_async_remote_copy(
+                        src_ref=zs.at[n * 2 + to],
+                        dst_ref=zr.at[n],
+                        send_sem=zsend.at[n],
+                        recv_sem=zrecv.at[n],
+                        device_id=away(dz, (dz + t) % 4, dc),
+                        device_id_type=MESH,
+                    )
+                    copy.start()
+                    pieces.append(copy)
+                else:
+                    zr[0] = zs[to]
+    for copy in pieces:
+        copy.wait_recv()
+    for dc in range(2):
+        e = 1 - core if dc else core
+        for odd in range(2):
+            half = lax.rem(x + odd, 2)
+            total = None
+            for n, (dz, dx, c) in enumerate(shifts):
+                if c == dc and dx % 2 == odd:
+                    total = zr[n].astype(F32) if total is None else total + zr[n].astype(F32)
+            out_ref[e, :, pl.ds(pl.multiple_of(half * HALF, HALF), HALF)] = total[:, :HALF]
+            out_ref[e, :, pl.ds(pl.multiple_of(IMG + half * HALF, HALF), HALF)] = total[:, HALF:]
+    for copy in rows + pieces:
+        copy.wait_send()
+
+
+def reduced(part):
+    vm = pl.BlockSpec(memory_space=pltpu.VMEM)
+    return pl.pallas_call(
+        reduce_kernel,
+        in_specs=[vm],
+        out_specs=vm,
+        out_shape=jax.ShapeDtypeStruct((2, 32, 2 * IMG), F32),
+        scratch_shapes=[
+            pltpu.VMEM((4, 3, 4, YB, IMG), BF),
+            pltpu.VMEM((64, 32, IMG), BF),
+            pltpu.VMEM((32, 32, IMG), BF),
+            pltpu.SemaphoreType.DMA((4, 3)),
+            pltpu.SemaphoreType.DMA((4, 3)),
+            pltpu.SemaphoreType.DMA((32,)),
+            pltpu.SemaphoreType.DMA((32,)),
+        ],
+        compiler_params=pltpu.CompilerParams(collective_id=8, has_side_effects=True),
+        name="reduced",
+    )(part)
+
+
 def on_device(kspace, accept, trajectory, phase_coef, sens):
     zh, zl = lax.axis_index("zh"), lax.axis_index("zl")
     x, core = lax.axis_index("x"), lax.axis_index("core")
     half = lax.rem(x, 2)
 
-    kept = accept.reshape(4, 2, 4, 2, SHOTS).transpose(1, 3, 0, 2, 4).reshape(4, 128)
+    owner_zh, owner_x = np.arange(16) % 4, (np.arange(16) // 4 + np.arange(16)) % 4
+    listed = np.stack([owner_zh * 16 + (q // 2) * 8 + owner_x * 2 + q % 2 for q in range(4)]).astype(np.int32)
+    choice = (listed.reshape(-1)[:, None] == np.arange(DIRS)[None, :]).astype(np.float32)
+    kept = jnp.dot(jnp.asarray(choice), accept.astype(F32)).astype(jnp.int32).reshape(4, 128)
     upto = np.triu(np.ones((128, 128), np.float32))
     place = jnp.dot(kept.astype(F32), jnp.asarray(upto), preferred_element_type=F32).astype(jnp.int32) - 1
     place = jnp.where(kept > 0, place, -1)
@@ -318,7 +418,7 @@
     counts = jnp.sum(kept, axis=1)
     dir16, shot = order // SHOTS, order % SHOTS
     subset = jnp.arange(4)[:, None]
-    direction = (dir16 // 4) * 16 + (subset // 2) * 8 + (dir16 % 4) * 2 + subset % 2
+    direction = (dir16 % 4) * 16 + (subset // 2) * 8 + ((dir16 // 4 + dir16) % 4) * 2 + subset % 2
     source = direction * SHOTS + shot
     mine = zl * 2 + core
     meta = jnp.concatenate(
@@ -375,13 +475,7 @@
     level = sum((need > 2 * s).astype(jnp.int32) for s in LEVELS[:-1])
     part_image = lax.switch(level, [run(i, s) for i, s in enumerate(LEVELS)], flat, source, meta, sens_half, small, choose, basx)
 
-    rows = lax.all_to_all(part_image, "y", split_axis=0, concat_axis=0, tiled=True)
-    rows = jnp.sum(rows.astype(F32), 0).astype(BF)
-    rows = rows.reshape(16, 2, 32, IMG).reshape(32, 32, IMG)
-    pieces = lax.all_to_all(rows, ("zh", "x", "core"), split_axis=0, concat_axis=0, tiled=True)
-    pieces = pieces.reshape(4, 2, 2, 2, 32, 2, HALF).astype(F32)
-    total = jnp.sum(pieces, axis=(0, 1))
-    return total.transpose(1, 2, 3, 0, 4).reshape(2, 32, 2 * IMG)
+    return reduced(part_image)
 
 
 def solution(mesh):

time: 151 us -> 136 us (0.901)
  the two profiles are of different devices: /device:TPU:33 before, /device:TPU:1 now
where the time goes in v3:
time: 136 us; the launch traced here: 135 us
  Pallas kernels  124 us (91%)
  local copies, waits for them, and re-layouts  5.05 us (4%)
  other arithmetic  2.46 us (2%)
  matrix products  1.74 us (1%)
  between operations  1.4 us (1%)
    pallas_call x1, Pallas kernels, reduced(): pl.pallas_call(reduce_kernel, in_specs=[vm], out_specs=vm, out_shape=jax....  48 us
    pallas_call x1, Pallas kernels, exchange(): pl.pallas_call(functools.partial(exchange_kernel, slots), in_specs=[pl.Bl...  43.5 us
    pallas_call x1, Pallas kernels, gridded(): pl.pallas_call(functools.partial(image_kernel, slots), in_specs=[pl.Block...  32.9 us

profile of v3, /device:TPU:1, one launch (start us, length us, event | category | flops | bytes accessed | tf_op | source)
XLA Modules:
  0.0 135.4 jit_solution(17050135666242788239)
XLA Ops:
  0.0 0.0 copy-start
  0.0 0.7 convert_bitcast_fusion
  0.8 0.9 fusion.23
  1.6 0.1 reduce_sum.26
  1.7 0.1 reduce_sum.27
  1.8 0.6 dynamic_slice.28
  2.4 0.6 reduce_max.9
  4.4 0.1 copy.26
  4.5 0.1 gt.19
  4.6 0.1 copy.27
  4.7 0.1 convert_element_type.41
  4.8 0.9 fusion.1
  5.7 0.1 select_reduce_fusion
  5.8 0.1 fusion.9
  5.9 0.6 pad_add_fusion.1
  6.6 0.0 copy-done
  6.6 0.1 reshape.86
  6.7 0.9 constant_dynamic-slice_fusion
  7.6 1.1 constant_dynamic-slice_fusion.3
  8.7 0.1 pad_maximum_fusion
  8.8 77.0 %conditional.1 = (bf16[4,16,64,256]{3,2,1,0:T(8,128)(2,1)S(1)}) conditional(s32[]{:T(128)} %clamp.3, (s32[4,96]{1,0:T(4,128)S(1)}, bf16[512,512]{1,0:T(8,128)(2,1)}, f32[24,128]{1,0:T(8,128)S(1)}, bf16[512,4,4,512]{3,2,1,0:T(4,128)(2,1)}, bf16[4,256,256]{2,1,0:T(8,128)(2,1)S(1)}, /*index=5*/s32[104]{0:T(128)S(1)}, ...), branch_computations={%region_4.5_spmd, %region_5.6_spmd, %region_6.7_spmd} | conditional | flops 16106127360 | bytes 59974748 | solution.py:476
  8.8 0.1 copy.30
  8.9 0.1 copy.24
  9.0 0.1 reshape.81.idx_ref
  9.1 0.0 copy-start.3
  9.1 0.0 copy-start.6
  9.1 43.5 %exchange.4 = (bf16[2,4,2,36,16,256]{5,4,3,2,1,0:T(8,128)(2,1)S(1)}, bf16[2,4,256,256]{3,2,1,0:T(8,128)(2,1)S(1)}, f32[16,24,128]{2,1,0:T(8,128)S(1)}) custom-call(s32[288]{0:T(512)S(1)} %reshape.81.idx_ref, bf16[512,512]{1,0:T(8,128)(2,1)} %get-tuple-element.84.tab_ref, f32[24,128]{1,0:T(8,128)S(1)} %get-tuple-element.85.small_ref, ...), custom_call_target="tpu_custom_call" | custom-call | flops 2415919104 | bytes 16777216 | tf_op jit(solution)/shard_map/cond/branch_1_fun/exchange/pallas_call | solution.py:176
  52.6 0.0 copy-done.3
  52.6 0.0 copy-done.6
  52.6 32.9 %gridded.4 = bf16[4,16,64,256]{3,2,1,0:T(8,128)(2,1)S(1)} custom-call(s32[104]{0:T(128)S(1)} %get-tuple-element.82.meta_ref, bf16[2,4,2,36,16,256]{5,4,3,2,1,0:T(8,128)(2,1)S(1)} %get-tuple-element.88.data_ref, bf16[2,4,256,256]{3,2,1,0:T(8,128)(2,1)S(1)} %get-tuple-element.89.sens_ref, f32[16,24,128]{2,1,0:T(8,128)S(1)} %get-tuple-element.90.gath_ref, ...), custom_call_target="tpu_custom_call" | custom-call | flops 9663676416 | bytes 16777216 | tf_op jit(solution)/shard_map/cond/branch_1_fun/gridded/pallas_call | solution.py:288
  85.8 48.0 %reduced.1 = f32[2,32,512]{2,1,0:T(8,128)} custom-call(bf16[4,16,64,256]{3,2,1,0:T(8,128)(2,1)S(1)} %get-tuple-element.147.part_ref), custom_call_target="tpu_custom_call" | custom-call | tf_op jit(solution)/shard_map/reduced/pallas_call | solution.py:385
  133.8 1.6 %copy.36 = f32[2,32,512]{2,1,0:T(8,128)} copy(f32[2,32,512]{2,1,0:T(8,128)} %reduced.1) | data formatting | bytes 262144
  (11 shorter events, 0.1 us)
Async XLA Ops:
  0.0 6.6 %copy-start = (f32[2,8,16,16]{3,2,1,0:T(8,128)S(1)}, f32[2,8,16,16]{3,2,1,0:T(8,128)}, u32[]{:S(2)}) copy-start(f32[2,8,16,16]{3,2,1,0:T(8,128)} %param.17) | copy-start | bytes 49156
  9.1 43.5 %copy-start.3 = (bf16[2,256,256]{2,1,0:T(8,128)(2,1)S(1)}, bf16[2,256,256]{2,1,0:T(8,128)(2,1)}, u32[]{:S(2)}) copy-start(bf16[2,256,256]{2,1,0:T(8,128)(2,1)} %get-tuple-element.92.line_ref) | copy-start | bytes 786436 | tf_op jit(solution)/shard_map/cond
  9.1 43.5 %copy-start.6 = (bf16[256,96]{1,0:T(8,128)(2,1)S(1)}, bf16[256,96]{1,0:T(8,128)(2,1)}, u32[]{:S(2)}) copy-start(bf16[256,96]{1,0:T(8,128)(2,1)} %get-tuple-element.93.basy_ref) | copy-start | bytes 147460 | tf_op jit(solution)/shard_map/cond

commit v4 on v2

v4 whole, which is shorter than its diff:
```python
import functools
import math

import jax
import jax.numpy as jnp
import numpy as np
from jax import lax
from jax.experimental import pallas as pl
from jax.experimental.pallas import tpu as pltpu
from jax.sharding import Mesh, PartitionSpec as P

IMG = 256
SHOTS = 8
PB = 16
DIRS = 64
HALF = IMG // 2
MESH = pl.DeviceIdType.MESH
AXES = ("zh", "zl", "x", "y", "core")
BF = jnp.bfloat16
F32 = jnp.float32

LEVELS = (32, 36, 48)
CHUNKS = 4
YB = 64


def readout_const():
    k = np.arange(IMG)
    ang = (np.outer(k, k) % IMG).astype(np.float64) * (2.0 * np.pi / IMG)
    c, s = np.cos(ang).astype(np.float32), np.sin(ang).astype(np.float32)
    tab = np.concatenate([np.concatenate([c, s], 1), np.concatenate([-s, c], 1)], 0)
    order = np.concatenate([np.arange(HALF), IMG + np.arange(HALF), HALF + np.arange(HALF), IMG + HALF + np.arange(HALF)])
    return jnp.asarray(tab[:, order]).astype(BF)


def line_const():
    k = np.arange(IMG)
    ang = (np.outer(k, k) % IMG).astype(np.float64) * (2.0 * np.pi / IMG)
    return jnp.asarray(np.concatenate([np.cos(ang), np.sin(ang)], 1).astype(np.float32)).astype(BF)


def basis_const():
    points = np.arange(IMG, dtype=np.float64)
    orders = np.arange(PB, dtype=np.float64)
    return np.cos(np.pi * orders[None, :] * (points[:, None] + 0.5) / IMG)


def split3(a):
    one = np.asarray(a, np.float32).astype(BF)
    rest = np.asarray(a, np.float64) - one.astype(np.float64)
    two = rest.astype(np.float32).astype(BF)
    rest = rest - two.astype(np.float64)
    return one, two, rest.astype(np.float32).astype(BF)


def poly_consts():
    u = np.cos(np.linspace(0, np.pi, 4001)) * 0.125 + 0.125
    t = np.sqrt(np.maximum(u, 0))
    fs = np.where(t > 1e-9, np.sin(2 * np.pi * t) / np.where(t > 1e-9, t, 1), 2 * np.pi)
    return [float(v) for v in np.polyfit(u, fs, 5)], [float(v) for v in np.polyfit(u, np.cos(2 * np.pi * t), 6)]


SIN_C, COS_C = poly_consts()


def sincos_turns(turns):
    t = turns - jnp.round(turns)
    u = t * t
    s = jnp.full_like(u, SIN_C[0])
    for v in SIN_C[1:]:
        s = s * u + v
    c = jnp.full_like(u, COS_C[0])
    for v in COS_C[1:]:
        c = c * u + v
    return s * t, c


def partner(p, i, n):
    if p == 0:
        return i + 1 - 2 * lax.rem(i, 2)
    return lax.rem(i + 2 * lax.rem(i, 2) - 1 + n, n)


def split_bf16(a):
    one = a.astype(BF)
    rest = a - one.astype(F32)
    two = rest.astype(BF)
    return one, two, (rest - two.astype(F32)).astype(BF)


def kernel(slots, idx_ref, meta_ref, take_ref, weight_ref, tab_ref, small_ref, choose_ref, line_ref, basy_ref, basx_ref, kspace_ref,
           sens_ref, out_ref, kv, send, recv, both, gath, contrib, sens, weights_a, weights_b, traj, mixes, relay_out,
           relay_in, block_out, block_in, zs, zr, load_sem, local_sem, self_sem, send_sem, recv_sem, spread_send, spread_recv,
           relay_sems, block_sems, zsend, zrecv):
    zh, zl = lax.axis_index("zh"), lax.axis_index("zl")
    x, y, core = lax.axis_index("x"), lax.axis_index("y"), lax.axis_index("core")
    z = zh * 2 + zl
    half = lax.rem(x, 2)
    src = half * 2 + zl
    part = slots // CHUNKS

    load = pltpu.make_async_copy(kspace_ref, kv, load_sem)
    load.start()
    own_sens = pltpu.make_async_copy(sens_ref, both.at[core], local_sem.at[0])
    own_sens.start()

    def target(p, bits):
        bx, bz, bc = bits
        tx = partner(p, x, 4) if bx else x
        tz = partner(p, z, 8) if bz else z
        tc = 1 - core if bc else core
        return tz // 2, lax.rem(tz, 2), tx, y, tc

    def far(dz, dx, dc=0):
        return (lax.rem(zh + dz, 4), zl, lax.rem(x + dx, 4), y, 1 - core if dc else core)

    def along(r):
        return (zh, zl, x, lax.rem(y + r, 4), core)

    groups = [(bz, bc, p) for bz in (1, 0) for bc in (0, 1) for p in (0, 1)]
    every = [(g, p, (bx, bz, bc)) for g, (bz, bc, p) in enumerate(groups) for bx in (1, 0) if bx + bz + bc]
    spread = [(dz, dx) for dz in range(4) for dx in range(4) if dz + dx]
    shifts = [(dz, (dz + t) % 4, dc) for t in range(4) for dz in range(4) for dc in range(2)]
    core_peer = (zh, zl, x, y, 1 - core)

    barrier = pltpu.get_barrier_semaphore()
    for _, p, bits in every:
        pl.semaphore_signal(barrier, inc=1, device_id=target(p, bits), device_id_type=MESH)
    for shift in shifts[1:]:
        pl.semaphore_signal(barrier, inc=1, device_id=far(*shift), device_id_type=MESH)
    for r in (1, 3):
        pl.semaphore_signal(barrier, inc=1, device_id=along(r), device_id_type=MESH)
    pl.semaphore_wait(barrier, len(every) + len(shifts) - 1 + 2)

    def remote(src_ref, dst_ref, sems, n, where):
        return pltpu.make_async_remote_copy(
            src_ref=src_ref, dst_ref=dst_ref, send_sem=sems[0].at[n], recv_sem=sems[1].at[n],
            device_id=where, device_id_type=MESH,
        )

    place = lax.rem(x - zh + 4, 4) * 4 + zh
    spread_sems = (spread_send, spread_recv)
    first_copies = [remote(small_ref, gath.at[place], spread_sems, n, far(*shift)) for n, shift in enumerate(spread)]
    first_copies.append(remote(sens_ref, both.at[core], spread_sems, len(spread), core_peer))
    for copy in first_copies:
        copy.start()
    gath[place] = small_ref[...]

    def piece(c):
        return pl.ds(c * part, part)

    def chunk_copy(c, n):
        g, p, bits = every[n]
        column = 1 - half if bits[0] else half
        return pltpu.make_async_remote_copy(
            src_ref=send.at[g, column, piece(c)], dst_ref=recv.at[p, src, core, piece(c)],
            send_sem=send_sem.at[n, c], recv_sem=recv_sem.at[n, c], device_id=target(p, bits), device_id_type=MESH,
        )

    def self_copy(c, p):
        return pltpu.make_async_copy(send.at[4 + p, half, piece(c)], recv.at[p, src, core, piece(c)], self_sem.at[p, c])

    load.wait()

    def transform(c, carry):
        def one_group(g, carry):
            zb, cb = lax.rem(zl + 1 - g // 4, 2), lax.rem(core + lax.rem(g // 2, 2), 2)
            base = ((zb * 2 + cb) * 2 + lax.rem(g, 2)) * slots + c * part
            rows = jnp.concatenate([kv[idx_ref[base + i]].reshape(16, 2 * IMG) for i in range(part)], 0)
            spec = jnp.dot(rows, tab_ref[...], preferred_element_type=F32) * (1.0 / math.sqrt(IMG))
            spec = spec.astype(BF).reshape(part, 16, 2 * IMG)
            send[g, 0, piece(c)] = spec[:, :, :IMG]
            send[g, 1, piece(c)] = spec[:, :, IMG:]
            return carry

        lax.fori_loop(0, 8, one_group, 0)
        for n in range(len(every)):
            chunk_copy(c, n).start()
        for p in range(2):
            self_copy(c, p).start()
        return carry

    lax.fori_loop(0, CHUNKS, transform, 0)

    own_sens.wait()
    for copy in first_copies:
        copy.wait()
    scale = 1.0 / (math.sqrt(128.0) * SHOTS)
    for s in range(2):
        for c in range(4):
            sens[s, :, c * YB:(c + 1) * YB, :] = (both[s, c].astype(F32) * scale).reshape(4, YB, IMG)
    lines = jnp.dot(gath[:, :8, :].reshape(128, 128).astype(BF), choose_ref[...], preferred_element_type=F32)
    traj[0:128] = lines[:, :128].reshape(128, 1, 128)
    traj[128:256] = lines[:, 128:].reshape(128, 1, 128)
    one, two, three = split_bf16(gath[:, 8:, :].reshape(256, 128))
    flat6 = jnp.concatenate([one, one, two, two, one, three], 1)
    shot_row = lax.broadcasted_iota(jnp.int32, (128, 128), 0) // PB
    for s in range(SHOTS):
        b1, b2, b3 = [jnp.where(shot_row == s, basx_ref[i].astype(F32), 0.0).astype(BF) for i in range(3)]
        mixed = jnp.dot(flat6, jnp.concatenate([b1, b2, b1, b2, b3, b1], 0), preferred_element_type=F32)
        mixes[16 * s:16 * s + 16] = mixed.reshape(16, PB, 128)

    lane = lax.broadcasted_iota(jnp.int32, (1, HALF), 1)
    coil = lax.rem(lane // 4, 4)
    masks = [jnp.where(coil == c, 1.0, 0.0).astype(BF) for c in range(4)]
    first = lane < 64
    kline = lax.broadcasted_iota(jnp.int32, (IMG, HALF), 0).astype(F32)

    def prepare(j, p, weights):
        pick = jnp.where(kline == traj[meta_ref[j]], 1.0, 0.0).astype(BF)
        cosine = jnp.dot(line_ref[0], pick, preferred_element_type=F32)
        sine = jnp.dot(line_ref[1], pick, preferred_element_type=F32)
        table = jnp.where(first, cosine, sine).astype(BF)
        for c in range(4):
            weights[:, c * YB:(c + 1) * YB, :] = (table * masks[c]).reshape(4, YB, HALF)

    def combine(j, p, slot, weights):
        one, two, three = split_bf16(mixes[meta_ref[104 + j]])
        mixed6 = jnp.concatenate([one, two, one, two, three, one], 0)
        rhs = []
        for s in range(2):
            rows = jnp.concatenate([recv[p, w, s, slot] for w in range(4)], 0)
            swapped = jnp.concatenate([-rows[:, HALF:], rows[:, :HALF]], 1)
            rhs.append(jnp.concatenate([rows, swapped], 0))
        for b in range(IMG // YB):
            turns = jnp.dot(basy_ref[b * YB:(b + 1) * YB, :], mixed6, preferred_element_type=F32)
            sine, cosine = sincos_turns(turns)
            ure = uim = None
            for s in range(2):
                image = jnp.dot(weights[b], rhs[s], preferred_element_type=F32)
                for c in range(4):
                    ire, iim = image[c * YB:(c + 1) * YB, :HALF], image[c * YB:(c + 1) * YB, HALF:]
                    sre = sens[s, b, c * YB:(c + 1) * YB, :HALF]
                    sim = sens[s, b, c * YB:(c + 1) * YB, HALF:]
                    re = sre * ire + sim * iim
                    im = sre * iim - sim * ire
                    ure = re if ure is None else ure + re
                    uim = im if uim is None else uim + im
            contrib[j, b, :, :HALF] = cosine * ure + sine * uim
            contrib[j, b, :, HALF:] = cosine * uim - sine * ure

    prepare(0, 0, weights_a)

    def work(c, carry):
        for n in range(len(every)):
            chunk_copy(c, n).wait_recv()
        for p in range(2):
            self_copy(c, p).wait()

        def pair(k, carry):
            i = c * part + k
            prepare(2 * i + 1, 1, weights_b)
            combine(2 * i, 0, i, weights_a)
            prepare(2 * i + 2, 0, weights_a)
            combine(2 * i + 1, 1, i, weights_b)
            return carry

        lax.fori_loop(0, part, pair, 0)
        return carry

    lax.fori_loop(0, CHUNKS, work, 0)

    def shots(o, b):
        total = None
        for s in range(6):
            term = contrib[take_ref[o * 6 + s], b] * weight_ref[o * 6 + s]
            total = term if total is None else total + term
        return total

    def group(t):
        return lax.rem(x - zh + t + 4, 4) * 4

    ring = ((1, 0), (3, 2))
    relays, blocks, pieces = [], [], []
    for t in range(4):
        for way, (r, k0) in enumerate(ring):
            for k in range(2):
                relay_out[t, way, k] = shots(group(t) + k0 + k, lax.rem(y + 2, 4)).astype(BF)
            copy = remote(relay_out.at[t, way], relay_in.at[t, way], relay_sems, t * 2 + way, along(r))
            copy.start()
            relays.append(copy)
    for t in range(4):
        for way, (r, k0) in enumerate(ring):
            there = lax.rem(y + r, 4)
            relays[t * 2 + way].wait_recv()
            for k in range(4):
                total = shots(group(t) + k, there)
                if k0 <= k < k0 + 2:
                    total = total + relay_in[t, way, k - k0].astype(F32)
                block_out[t, way, k] = total.astype(BF)
            copy = remote(block_out.at[t, way], block_in.at[t, way], block_sems, t * 2 + way, along(r))
            copy.start()
            blocks.append(copy)
    for t in range(4):
        blocks[t * 2].wait_recv()
        blocks[t * 2 + 1].wait_recv()
        for dz in range(4):
            there = lax.rem(zh + dz, 4)
            total = shots(group(t) + there, y) + block_in[t, 0, there].astype(F32) + block_in[t, 1, there].astype(F32)
            for dc in range(2):
                n = (t * 4 + dz) * 2 + dc
                zs[n * 2:n * 2 + 2] = total.astype(BF).reshape(2, 32, IMG)
                to = 1 - core if dc else core
                if n:
                    copy = remote(zs.at[n * 2 + to], zr.at[n], (zsend, zrecv), n, far(dz, (dz + t) % 4, dc))
                    copy.start()
                    pieces.append(copy)
                else:
                    zr[0] = zs[to]
    for copy in pieces:
        copy.wait_recv()
    for dc in range(2):
        e = 1 - core if dc else core
        for odd in range(2):
            column = lax.rem(x + odd, 2)
            total = None
            for n, (dz, dx, c) in enumerate(shifts):
                if c == dc and dx % 2 == odd:
                    total = zr[n].astype(F32) if total is None else total + zr[n].astype(F32)
            out_ref[e, :, pl.ds(pl.multiple_of(column * HALF, HALF), HALF)] = total[:, :HALF]
            out_ref[e, :, pl.ds(pl.multiple_of(IMG + column * HALF, HALF), HALF)] = total[:, HALF:]
    for copy in relays + blocks + pieces:
        copy.wait_send()

    def sent(c, carry):
        for n in range(len(every)):
            chunk_copy(c, n).wait_send()
        return carry

    lax.fori_loop(0, CHUNKS, sent, 0)


def combined(slots, ident, index, meta, take, weight, tab, small, choose, line, basy, basx, kspace, sens):
    any_ = pl.BlockSpec(memory_space=pl.ANY)
    vm = pl.BlockSpec(memory_space=pltpu.VMEM)
    sm = pl.BlockSpec(memory_space=pltpu.SMEM)
    dma = pltpu.SemaphoreType.DMA
    return pl.pallas_call(
        functools.partial(kernel, slots),
        in_specs=[sm, sm, sm, sm] + [vm] * 6 + [any_, any_],
        out_specs=vm,
        out_shape=jax.ShapeDtypeStruct((2, 32, 2 * IMG), F32),
        scratch_shapes=[
            pltpu.VMEM((DIRS * SHOTS, 4, 4, 2 * IMG), BF),
            pltpu.VMEM((8, 2, slots, 16, IMG), BF),
            pltpu.VMEM((2, 4, 2, slots, 16, IMG), BF),
            pltpu.VMEM((2, 4, IMG, IMG), BF),
            pltpu.VMEM((16, 24, 128), F32),
            pltpu.VMEM((2 * slots, 4, YB, IMG), F32),
            pltpu.VMEM((2, 4, 4 * YB, IMG), F32),
            pltpu.VMEM((4, 4 * YB, HALF), BF),
            pltpu.VMEM((4, 4 * YB, HALF), BF),
            pltpu.VMEM((256, 1, 128), F32),
            pltpu.VMEM((128, PB, 128), F32),
            pltpu.VMEM((4, 2, 2, YB, IMG), BF),
            pltpu.VMEM((4, 2, 2, YB, IMG), BF),
            pltpu.VMEM((4, 2, 4, YB, IMG), BF),
            pltpu.VMEM((4, 2, 4, YB, IMG), BF),
            pltpu.VMEM((64, 32, IMG), BF),
            pltpu.VMEM((32, 32, IMG), BF),
            dma,
            dma((1,)),
            dma((2, CHUNKS)),
            dma((14, CHUNKS)),
            dma((14, CHUNKS)),
            dma((16,)),
            dma((16,)),
            [dma((8,)), dma((8,))],
            [dma((8,)), dma((8,))],
            dma((32,)),
            dma((32,)),
        ],
        compiler_params=pltpu.CompilerParams(collective_id=ident, has_side_effects=True, vmem_limit_bytes=67000000),
        cost_estimate=pl.CostEstimate(flops=2 * slots * 4096 * 256 * 256, bytes_accessed=16 << 20, transcendentals=0),
        name="combined",
    )(index, meta, take, weight, tab, small, choose, line, basy, basx, kspace, sens)


def on_device(kspace, accept, trajectory, phase_coef, sens):
    zh, zl = lax.axis_index("zh"), lax.axis_index("zl")
    x, core = lax.axis_index("x"), lax.axis_index("core")
    half = lax.rem(x, 2)

    owner_zh, owner_x = np.arange(16) % 4, (np.arange(16) // 4 + np.arange(16)) % 4
    listed = np.stack([owner_zh * 16 + (q // 2) * 8 + owner_x * 2 + q % 2 for q in range(4)]).astype(np.int32)
    choice = (listed.reshape(-1)[:, None] == np.arange(DIRS)[None, :]).astype(np.float32)
    kept = jnp.dot(jnp.asarray(choice), accept.astype(F32)).astype(jnp.int32).reshape(4, 128)
    upto = np.triu(np.ones((128, 128), np.float32))
    upto_count = jnp.dot(kept.astype(F32), jnp.asarray(upto), preferred_element_type=F32).astype(jnp.int32)
    place = jnp.where(kept > 0, upto_count - 1, -1)
    unit = jnp.arange(128, dtype=jnp.int32)
    order = jnp.sum(jnp.where(place[:, None, :] == jnp.arange(96)[None, :, None], unit[None, None, :], 0), 2)
    counts = jnp.sum(kept, axis=1)
    dir16, shot = order // SHOTS, order % SHOTS
    subset = jnp.arange(4)[:, None]
    direction = (dir16 % 4) * 16 + (subset // 2) * 8 + ((dir16 // 4 + dir16) % 4) * 2 + subset % 2
    source = direction * SHOTS + shot
    mine = zl * 2 + core
    kept16 = lax.dynamic_index_in_dim(kept, mine, 0, False).reshape(16, SHOTS)
    starts = lax.dynamic_index_in_dim(upto_count, mine, 0, False).reshape(16, SHOTS)[:, 0] - kept16[:, 0]
    codes = jnp.concatenate([lax.dynamic_index_in_dim(order, mine, 0, False), jnp.zeros((8,), jnp.int32)])
    meta = jnp.concatenate([codes + 128 * (jnp.arange(104) % 2), (codes % SHOTS) * 16 + codes // SHOTS])
    take = (starts[:, None] + jnp.arange(6)[None, :]).reshape(96)
    weight = (jnp.arange(6)[None, :] < jnp.sum(kept16, 1, keepdims=True)).astype(F32).reshape(96)

    small = jnp.concatenate(
        [
            lax.dynamic_index_in_dim(trajectory, core, 0, False).astype(F32),
            lax.dynamic_index_in_dim(phase_coef, core, 0, False).transpose(1, 0, 2).reshape(PB, SHOTS * PB),
        ],
        0,
    )
    k = jnp.arange(128)
    w, row = (k // 16) % 4, k % 4
    wx, wz = w // 2, w % 2
    z = zh * 2 + zl
    picks = []
    for p in range(2):
        rx = jnp.where(wx == x % 2, x, partner(p, x, 4))
        rz = jnp.where(wz == z % 2, z, partner(p, z, 8))
        picks.append((rz * 4 + rx) * 4 + row)
    choose = (jnp.arange(128)[:, None] == jnp.concatenate(picks)[None, :]).astype(BF)

    basis = basis_const()
    b1, b2, b3 = split3(basis / (2.0 * math.pi))
    basy = jnp.asarray(np.concatenate([b1, b1, b2, b2, b1, b3], 1))
    basx = jnp.asarray(np.stack([np.tile(np.asarray(part).T, (SHOTS, 1)) for part in split3(basis)]))
    basx = lax.dynamic_slice_in_dim(basx, half * HALF, HALF, 2)
    sens_half = jnp.concatenate(
        [
            lax.dynamic_slice_in_dim(sens, half * HALF, HALF, 2),
            lax.dynamic_slice_in_dim(sens, IMG + half * HALF, HALF, 2),
        ],
        2,
    )
    tab = readout_const()
    line = jnp.stack(jnp.split(line_const(), 2, 1))
    flat = kspace.reshape(DIRS * SHOTS, 4, 4, 2 * IMG)

    def run(ident, slots):
        def branch(flat, source, meta, take, weight, sens_half, small, choose, basx):
            take = jnp.minimum(take, 2 * slots - 1)
            index = source[:, : 2 * slots].reshape(4, slots, 2).transpose(0, 2, 1).reshape(-1)
            return combined(slots, ident, index, meta, take, weight, tab, small, choose, line, basy, basx, flat, sens_half)

        return branch

    need = jnp.max(counts)
    level = sum((need > 2 * s).astype(jnp.int32) for s in LEVELS[:-1])
    return lax.switch(
        level, [run(i, s) for i, s in enumerate(LEVELS)], flat, source, meta, take, weight, sens_half, small, choose, basx
    )


def solution(mesh):
    inner = Mesh(mesh.devices.reshape(4, 2, 4, 4, 2), AXES)
    return jax.shard_map(
        on_device,
        mesh=inner,
        in_specs=(
            P(None, None, ("y", "core"), ("zh", "zl", "x"), None),
            P(),
            P(("zh", "zl", "x"), None, None),
            P(("zh", "zl", "x"), None, None, None),
            P(("y", "core"), None, None),
        ),
        out_specs=P(("zh", "zl", "x"), ("y", "core"), None),
        check_vma=False,
    )
```

time: 151 us -> 117 us (0.77)
  the two profiles are of different devices: /device:TPU:33 before, /device:TPU:1 now
where the time goes in v4:
time: 117 us
  Pallas kernels  100 us (85%)
  local copies, waits for them, and re-layouts  9.35 us (8%)
  other arithmetic  3.7 us (3%)
  matrix products  1.74 us (1%)
  between operations  1.43 us (1%)
    pallas_call x1, Pallas kernels, combined(): pl.pallas_call(functools.partial(kernel, slots), in_specs=[sm, sm, sm, sm...  100 us

profile of v4, /device:TPU:1, one launch (start us, length us, event | category | flops | bytes accessed | tf_op | source)
XLA Modules:
  0.0 116.9 jit_solution(10197504212078865810)
XLA Ops:
  0.0 1.1 constant_dynamic-slice_fusion.3
  1.1 0.9 pad_maximum_fusion
  2.0 0.6 fusion.31
  2.6 0.9 fusion.49
  3.4 0.1 copy.57
  3.5 0.1 reshape.104
  3.6 0.9 add_select_fusion.7
  4.5 0.2 select_reduce_fusion
  4.7 0.1 pad_add_fusion
  4.8 0.1 reshape.106
  4.9 0.9 dynamic-slice_bitcast_fusion
  5.8 0.1 reshape.107
  5.9 0.7 convert_bitcast_fusion
  6.7 0.1 reduce_sum.35
  6.8 0.1 reduce_sum.36
  6.9 0.6 reduce_max.9
  8.8 106.5 %conditional.1 = (f32[2,32,512]{2,1,0:T(8,128)}) conditional(s32[]{:T(128)} %clamp.3, (s32[4,96]{1,0:T(4,128)S(1)}, s32[4,128]{1,0:T(4,128)S(1)}, s32[208]{0:T(256)S(1)}, s32[16,6]{1,0:T(8,128)S(1)}, bf16[512,512]{1,0:T(8,128)(2,1)}, /*index=5*/f32[24,128]{1,0:T(8,128)S(1)}, bf16[128,256]{1,0:T(8,128)(2,1)}, ...), branch_computations={%region_5.6_spmd.clone, %region_6.7_spmd.clone, %region_7.8_spmd.c... | conditional | flops 25769811968 | bytes 17052852 | solution.py:450
  9.0 0.1 copy.81
  9.2 0.1 copy.74
  9.3 0.1 copy.83
  9.4 0.1 copy.85
  9.5 0.1 copy.86
  9.6 0.1 copy.88
  9.7 0.1 copy.80
  9.8 0.1 copy.87
  10.0 0.1 copy.75
  10.1 0.1 copy.76
  10.2 0.1 copy.77
  10.3 0.1 copy.82
  10.4 0.1 copy.84
  10.5 0.1 copy.78
  10.7 0.1 copy.55
  10.7 0.7 reshape.120.idx_ref
  11.4 1.7 %constant_dynamic-slice_fusion.1.basx_ref = bf16[3,128,128]{2,1,0:T(8,128)(2,1)} fusion(bf16[3,128,256]{2,1,0:T(8,128)(2,1)} %constant.251.clone.5, s32[]{:T(128)S(6)} %select_n.197), kind=kLoop, calls=%fused_computation.50 | loop fusion | bytes 196612 | tf_op jit(solution)/shard_map/dynamic_slice | solution.py:428
  13.1 0.1 reshape.122
  13.2 0.1 fusion.16
  13.3 0.1 add_minimum_fusion.1
  13.4 0.6 reshape.131.take_ref
  14.0 0.1 reduce_sum.43
  14.1 0.1 compare_convert_fusion.1
  14.2 0.7 reshape.132.weight_ref
  14.9 100.0 %combined.4 = f32[2,32,512]{2,1,0:T(8,128)} custom-call(s32[288]{0:T(512)} %reshape.120.idx_ref, s32[208]{0:T(256)S(1)} %get-tuple-element.527.meta_ref, s32[96]{0:T(128)} %reshape.131.take_ref, f32[96]{0:T(128)} %reshape.132.weight_ref, bf16[512,512]{1,0:T(8,128)(2,1)} %get-tuple-element.528.tab_ref, f32[24,128]{1,0:T(8,128)S(1)} %get-tuple-element.529.small_ref, ...), custom_call_target="tpu_custom_call" | custom-call | flops 19327352832 | bytes 16777216 | tf_op jit(solution)/shard_map/cond/branch_1_fun/combined/pallas_call | solution.py:338
  115.3 1.6 %copy.111 = f32[2,32,512]{2,1,0:T(8,128)} copy(f32[2,32,512]{2,1,0:T(8,128)} %get-tuple-element.117) | data formatting | bytes 262144
  (24 shorter events, 0.3 us)

commit v5 on v4

--- a/solution.py
+++ b/solution.py
@@ -88,8 +88,7 @@
     return one, two, (rest - two.astype(F32)).astype(BF)
 
 
-def kernel(slots, idx_ref, meta_ref, take_ref, weight_ref, tab_ref, small_ref, choose_ref, line_ref, basy_ref, basx_ref, kspace_ref,
-           sens_ref, out_ref, kv, send, recv, both, gath, contrib, sens, weights_a, weights_b, traj, mixes, relay_out,
+def kernel(slots, plan_ref, traj_ref, coef_ref, tab_ref, line_ref, basy_ref, basx_ref, kspace_ref, sens_ref, out_ref, small, kv, send, recv, both, gath, contrib, sens, weights_a, weights_b, traj, mixes, relay_out,
            relay_in, block_out, block_in, zs, zr, load_sem, local_sem, self_sem, send_sem, recv_sem, spread_send, spread_recv,
            relay_sems, block_sems, zsend, zrecv):
     zh, zl = lax.axis_index("zh"), lax.axis_index("zl")
@@ -101,8 +100,13 @@
 
     load = pltpu.make_async_copy(kspace_ref, kv, load_sem)
     load.start()
-    own_sens = pltpu.make_async_copy(sens_ref, both.at[core], local_sem.at[0])
-    own_sens.start()
+    sens_parts = [
+        (sens_ref.at[:, :, pl.ds(pl.multiple_of(k * IMG + half * HALF, HALF), HALF)], both.at[core, :, :, k * HALF:(k + 1) * HALF])
+        for k in range(2)
+    ]
+    own_sens = [pltpu.make_async_copy(a, b, local_sem.at[k]) for k, (a, b) in enumerate(sens_parts)]
+    for copy in own_sens:
+        copy.start()
 
     def target(p, bits):
         bx, bz, bc = bits
@@ -119,9 +123,21 @@
 
     groups = [(bz, bc, p) for bz in (1, 0) for bc in (0, 1) for p in (0, 1)]
     every = [(g, p, (bx, bz, bc)) for g, (bz, bc, p) in enumerate(groups) for bx in (1, 0) if bx + bz + bc]
+    turn = [(bx, bz, bc, p) for bc in (0, 1) for bx, bz in ((1, 1), (0, 1), (1, 0)) for p in (0, 1)] + [(0, 0, 1, 0), (0, 0, 1, 1)]
+    order = [[(b[0], b[1], b[2], p) for _, p, b in every].index(entry) for entry in turn]
     spread = [(dz, dx) for dz in range(4) for dx in range(4) if dz + dx]
     shifts = [(dz, (dz + t) % 4, dc) for t in range(4) for dz in range(4) for dc in range(2)]
     core_peer = (zh, zl, x, y, 1 - core)
+
+    small[0:SHOTS] = traj_ref[core].astype(F32)
+    term = lax.broadcasted_iota(jnp.int32, (PB, 128), 0)
+    place_lane = lax.broadcasted_iota(jnp.int32, (PB, 128), 1)
+    spread_out = None
+    for s in range(SHOTS):
+        where = (place_lane == s * PB + term).astype(F32)
+        moved = jnp.dot(coef_ref[core, s], where, preferred_element_type=F32, precision=lax.Precision.HIGHEST)
+        spread_out = moved if spread_out is None else spread_out + moved
+    small[SHOTS:] = spread_out
 
     barrier = pltpu.get_barrier_semaphore()
     for _, p, bits in every:
@@ -140,11 +156,12 @@
 
     place = lax.rem(x - zh + 4, 4) * 4 + zh
     spread_sems = (spread_send, spread_recv)
-    first_copies = [remote(small_ref, gath.at[place], spread_sems, n, far(*shift)) for n, shift in enumerate(spread)]
-    first_copies.append(remote(sens_ref, both.at[core], spread_sems, len(spread), core_peer))
+    first_copies = [remote(small, gath.at[place], spread_sems, n, far(*shift)) for n, shift in enumerate(spread)]
+    for k, (a, b) in enumerate(sens_parts):
+        first_copies.append(remote(a, b, spread_sems, len(spread) + k, core_peer))
     for copy in first_copies:
         copy.start()
-    gath[place] = small_ref[...]
+    gath[place] = small[...]
 
     def piece(c):
         return pl.ds(c * part, part)
@@ -165,8 +182,8 @@
     def transform(c, carry):
         def one_group(g, carry):
             zb, cb = lax.rem(zl + 1 - g // 4, 2), lax.rem(core + lax.rem(g // 2, 2), 2)
-            base = ((zb * 2 + cb) * 2 + lax.rem(g, 2)) * slots + c * part
-            rows = jnp.concatenate([kv[idx_ref[base + i]].reshape(16, 2 * IMG) for i in range(part)], 0)
+            base = c * part * 2 + lax.rem(g, 2)
+            rows = jnp.concatenate([kv[plan_ref[zb * 2 + cb, base + 2 * i]].reshape(16, 2 * IMG) for i in range(part)], 0)
             spec = jnp.dot(rows, tab_ref[...], preferred_element_type=F32) * (1.0 / math.sqrt(IMG))
             spec = spec.astype(BF).reshape(part, 16, 2 * IMG)
             send[g, 0, piece(c)] = spec[:, :, :IMG]
@@ -174,7 +191,7 @@
             return carry
 
         lax.fori_loop(0, 8, one_group, 0)
-        for n in range(len(every)):
+        for n in order:
             chunk_copy(c, n).start()
         for p in range(2):
             self_copy(c, p).start()
@@ -182,21 +199,30 @@
 
     lax.fori_loop(0, CHUNKS, transform, 0)
 
-    own_sens.wait()
+    for copy in own_sens:
+        copy.wait()
     for copy in first_copies:
         copy.wait()
     scale = 1.0 / (math.sqrt(128.0) * SHOTS)
     for s in range(2):
         for c in range(4):
             sens[s, :, c * YB:(c + 1) * YB, :] = (both[s, c].astype(F32) * scale).reshape(4, YB, IMG)
-    lines = jnp.dot(gath[:, :8, :].reshape(128, 128).astype(BF), choose_ref[...], preferred_element_type=F32)
-    traj[0:128] = lines[:, :128].reshape(128, 1, 128)
-    traj[128:256] = lines[:, 128:].reshape(128, 1, 128)
-    one, two, three = split_bf16(gath[:, 8:, :].reshape(256, 128))
+    k = lax.broadcasted_iota(jnp.int32, (1, 128), 1)
+    wx, wz = lax.rem(k // 32, 2), lax.rem(k // 16, 2)
+    line_numbers = gath[:, :SHOTS, :].reshape(128, 128).astype(BF)
+    for p in range(2):
+        rx = jnp.where(wx == half, x, partner(p, x, 4))
+        rz = jnp.where(wz == zl, z, partner(p, z, 8))
+        wanted = (rz * 4 + rx) * 4 + lax.rem(k, 4)
+        choose = (lax.broadcasted_iota(jnp.int32, (128, 128), 0) == wanted).astype(F32).astype(BF)
+        lines = jnp.dot(line_numbers, choose, preferred_element_type=F32)
+        traj[128 * p:128 * p + 128] = lines.reshape(128, 1, 128)
+    one, two, three = split_bf16(gath[:, SHOTS:, :].reshape(256, 128))
     flat6 = jnp.concatenate([one, one, two, two, one, three], 1)
     shot_row = lax.broadcasted_iota(jnp.int32, (128, 128), 0) // PB
+    columns = pl.ds(pl.multiple_of(half * HALF, HALF), HALF)
     for s in range(SHOTS):
-        b1, b2, b3 = [jnp.where(shot_row == s, basx_ref[i].astype(F32), 0.0).astype(BF) for i in range(3)]
+        b1, b2, b3 = [jnp.where(shot_row == s, basx_ref[i, :, columns].astype(F32), 0.0).astype(BF) for i in range(3)]
         mixed = jnp.dot(flat6, jnp.concatenate([b1, b2, b1, b2, b3, b1], 0), preferred_element_type=F32)
         mixes[16 * s:16 * s + 16] = mixed.reshape(16, PB, 128)
 
@@ -207,7 +233,7 @@
     kline = lax.broadcasted_iota(jnp.int32, (IMG, HALF), 0).astype(F32)
 
     def prepare(j, p, weights):
-        pick = jnp.where(kline == traj[meta_ref[j]], 1.0, 0.0).astype(BF)
+        pick = jnp.where(kline == traj[plan_ref[4, j]], 1.0, 0.0).astype(BF)
         cosine = jnp.dot(line_ref[0], pick, preferred_element_type=F32)
         sine = jnp.dot(line_ref[1], pick, preferred_element_type=F32)
         table = jnp.where(first, cosine, sine).astype(BF)
@@ -215,7 +241,7 @@
             weights[:, c * YB:(c + 1) * YB, :] = (table * masks[c]).reshape(4, YB, HALF)
 
     def combine(j, p, slot, weights):
-        one, two, three = split_bf16(mixes[meta_ref[104 + j]])
+        one, two, three = split_bf16(mixes[plan_ref[5, j]])
         mixed6 = jnp.concatenate([one, two, one, two, three, one], 0)
         rhs = []
         for s in range(2):
@@ -263,7 +289,7 @@
     def shots(o, b):
         total = None
         for s in range(6):
-            term = contrib[take_ref[o * 6 + s], b] * weight_ref[o * 6 + s]
+            term = contrib[plan_ref[6, o * SHOTS + s], b] * plan_ref[7, o * SHOTS + s].astype(F32)
             total = term if total is None else total + term
         return total
 
@@ -330,17 +356,18 @@
     lax.fori_loop(0, CHUNKS, sent, 0)
 
 
-def combined(slots, ident, index, meta, take, weight, tab, small, choose, line, basy, basx, kspace, sens):
+def combined(slots, ident, plan, traj, coefs, tab, line, basy, basx, kspace, sens):
     any_ = pl.BlockSpec(memory_space=pl.ANY)
     vm = pl.BlockSpec(memory_space=pltpu.VMEM)
     sm = pl.BlockSpec(memory_space=pltpu.SMEM)
     dma = pltpu.SemaphoreType.DMA
     return pl.pallas_call(
         functools.partial(kernel, slots),
-        in_specs=[sm, sm, sm, sm] + [vm] * 6 + [any_, any_],
+        in_specs=[sm] + [vm] * 6 + [any_, any_],
         out_specs=vm,
         out_shape=jax.ShapeDtypeStruct((2, 32, 2 * IMG), F32),
         scratch_shapes=[
+            pltpu.VMEM((24, 128), F32),
             pltpu.VMEM((DIRS * SHOTS, 4, 4, 2 * IMG), BF),
             pltpu.VMEM((8, 2, slots, 16, IMG), BF),
             pltpu.VMEM((2, 4, 2, slots, 16, IMG), BF),
@@ -359,12 +386,12 @@
             pltpu.VMEM((64, 32, IMG), BF),
             pltpu.VMEM((32, 32, IMG), BF),
             dma,
-            dma((1,)),
+            dma((2,)),
             dma((2, CHUNKS)),
             dma((14, CHUNKS)),
             dma((14, CHUNKS)),
-            dma((16,)),
-            dma((16,)),
+            dma((17,)),
+            dma((17,)),
             [dma((8,)), dma((8,))],
             [dma((8,)), dma((8,))],
             dma((32,)),
@@ -373,83 +400,83 @@
         compiler_params=pltpu.CompilerParams(collective_id=ident, has_side_effects=True, vmem_limit_bytes=67000000),
         cost_estimate=pl.CostEstimate(flops=2 * slots * 4096 * 256 * 256, bytes_accessed=16 << 20, transcendentals=0),
         name="combined",
-    )(index, meta, take, weight, tab, small, choose, line, basy, basx, kspace, sens)
+    )(plan, traj, coefs, tab, line, basy, basx, kspace, sens)
+
+
+def plan_kernel(accept_ref, plan_ref):
+    mine = lax.axis_index("zl") * 2 + lax.axis_index("core")
+
+    def iota(shape, axis):
+        return lax.broadcasted_iota(jnp.int32, shape, axis)
+
+    def flag(cond):
+        return jnp.where(cond, 1.0, 0.0)
+
+    tile = flag(lax.rem(iota((SHOTS, 128), 1), SHOTS) == iota((SHOTS, 128), 0)).astype(BF)
+    flags = jnp.dot(accept_ref[...].astype(F32).astype(BF), tile, preferred_element_type=F32)
+    lane = iota((1, 128), 1)
+    o, s = lane // SHOTS, lax.rem(lane, SHOTS)
+    first = lax.rem(o, 4) * 16 + lax.rem(o // 4 + o, 4) * 2
+    row = iota((8, 128), 0)
+    kept = jnp.zeros((8, 128), F32)
+    for q in range(4):
+        listed = iota((DIRS, 128), 0) == first + (q // 2) * 8 + q % 2
+        kept = kept + jnp.where(row == q, jnp.sum(jnp.where(listed, flags, 0.0), 0, keepdims=True), 0.0)
+    a, b = iota((128, 128), 0), iota((128, 128), 1)
+    keptb = kept.astype(BF)
+    upto = jnp.dot(keptb, flag(a <= b).astype(BF), preferred_element_type=F32)
+    total = jnp.dot(keptb, jnp.ones((128, 128), BF), preferred_element_type=F32)
+    count = jnp.dot(keptb, flag(a // SHOTS == b // SHOTS).astype(BF), preferred_element_type=F32)
+    begin = jnp.dot((upto - kept).astype(BF), flag(a == b // SHOTS * SHOTS).astype(BF), preferred_element_type=F32)
+    place = jnp.where(kept > 0.5, upto - 1.0, -1.0)
+    lanef = iota((128, 128), 0).astype(F32)
+
+    def packed(values, where):
+        return lax.dot_general(
+            values, flag(lanef == where), (((1,), (1,)), ((), ())), preferred_element_type=F32, precision=lax.Precision.HIGHEST
+        )
+
+    plan = jnp.zeros((8, 128), F32)
+    for q in range(4):
+        source = ((first + (q // 2) * 8 + q % 2) * SHOTS + s).astype(F32)
+        plan = plan + packed(jnp.where(row == q, source, 0.0), place[q:q + 1])
+
+    def own(v):
+        return jnp.sum(jnp.where(row == mine, v, 0.0), 0, keepdims=True)
+
+    codes = jnp.where(row == 4, lane, jnp.where(row == 5, s * 16 + o, 0)).astype(F32)
+    plan = plan + packed(codes, own(place))
+    plan = plan + jnp.where(row == 4, lax.rem(lane, 2) * 128, 0).astype(F32)
+    sf = s.astype(F32)
+    take = jnp.minimum(own(begin) + sf, own(total) - 1.0)
+    plan = plan + jnp.where(row == 6, take, 0.0) + jnp.where(row == 7, flag(sf < own(count)), 0.0)
+    plan_ref[0:8] = plan.astype(jnp.int32)
+    plan_ref[8:16] = jnp.broadcast_to(jnp.max(total, 0, keepdims=True), (8, 128)).astype(jnp.int32)
 
 
 def on_device(kspace, accept, trajectory, phase_coef, sens):
-    zh, zl = lax.axis_index("zh"), lax.axis_index("zl")
-    x, core = lax.axis_index("x"), lax.axis_index("core")
-    half = lax.rem(x, 2)
-
-    owner_zh, owner_x = np.arange(16) % 4, (np.arange(16) // 4 + np.arange(16)) % 4
-    listed = np.stack([owner_zh * 16 + (q // 2) * 8 + owner_x * 2 + q % 2 for q in range(4)]).astype(np.int32)
-    choice = (listed.reshape(-1)[:, None] == np.arange(DIRS)[None, :]).astype(np.float32)
-    kept = jnp.dot(jnp.asarray(choice), accept.astype(F32)).astype(jnp.int32).reshape(4, 128)
-    upto = np.triu(np.ones((128, 128), np.float32))
-    upto_count = jnp.dot(kept.astype(F32), jnp.asarray(upto), preferred_element_type=F32).astype(jnp.int32)
-    place = jnp.where(kept > 0, upto_count - 1, -1)
-    unit = jnp.arange(128, dtype=jnp.int32)
-    order = jnp.sum(jnp.where(place[:, None, :] == jnp.arange(96)[None, :, None], unit[None, None, :], 0), 2)
-    counts = jnp.sum(kept, axis=1)
-    dir16, shot = order // SHOTS, order % SHOTS
-    subset = jnp.arange(4)[:, None]
-    direction = (dir16 % 4) * 16 + (subset // 2) * 8 + ((dir16 // 4 + dir16) % 4) * 2 + subset % 2
-    source = direction * SHOTS + shot
-    mine = zl * 2 + core
-    kept16 = lax.dynamic_index_in_dim(kept, mine, 0, False).reshape(16, SHOTS)
-    starts = lax.dynamic_index_in_dim(upto_count, mine, 0, False).reshape(16, SHOTS)[:, 0] - kept16[:, 0]
-    codes = jnp.concatenate([lax.dynamic_index_in_dim(order, mine, 0, False), jnp.zeros((8,), jnp.int32)])
-    meta = jnp.concatenate([codes + 128 * (jnp.arange(104) % 2), (codes % SHOTS) * 16 + codes // SHOTS])
-    take = (starts[:, None] + jnp.arange(6)[None, :]).reshape(96)
-    weight = (jnp.arange(6)[None, :] < jnp.sum(kept16, 1, keepdims=True)).astype(F32).reshape(96)
-
-    small = jnp.concatenate(
-        [
-            lax.dynamic_index_in_dim(trajectory, core, 0, False).astype(F32),
-            lax.dynamic_index_in_dim(phase_coef, core, 0, False).transpose(1, 0, 2).reshape(PB, SHOTS * PB),
-        ],
-        0,
-    )
-    k = jnp.arange(128)
-    w, row = (k // 16) % 4, k % 4
-    wx, wz = w // 2, w % 2
-    z = zh * 2 + zl
-    picks = []
-    for p in range(2):
-        rx = jnp.where(wx == x % 2, x, partner(p, x, 4))
-        rz = jnp.where(wz == z % 2, z, partner(p, z, 8))
-        picks.append((rz * 4 + rx) * 4 + row)
-    choose = (jnp.arange(128)[:, None] == jnp.concatenate(picks)[None, :]).astype(BF)
+    vm = pl.BlockSpec(memory_space=pltpu.VMEM)
+    plan = pl.pallas_call(
+        plan_kernel, in_specs=[vm], out_specs=vm, out_shape=jax.ShapeDtypeStruct((16, 128), jnp.int32), name="plan"
+    )(accept)
 
     basis = basis_const()
     b1, b2, b3 = split3(basis / (2.0 * math.pi))
     basy = jnp.asarray(np.concatenate([b1, b1, b2, b2, b1, b3], 1))
     basx = jnp.asarray(np.stack([np.tile(np.asarray(part).T, (SHOTS, 1)) for part in split3(basis)]))
-    basx = lax.dynamic_slice_in_dim(basx, half * HALF, HALF, 2)
-    sens_half = jnp.concatenate(
-        [
-            lax.dynamic_slice_in_dim(sens, half * HALF, HALF, 2),
-            lax.dynamic_slice_in_dim(sens, IMG + half * HALF, HALF, 2),
-        ],
-        2,
-    )
     tab = readout_const()
     line = jnp.stack(jnp.split(line_const(), 2, 1))
     flat = kspace.reshape(DIRS * SHOTS, 4, 4, 2 * IMG)
 
     def run(ident, slots):
-        def branch(flat, source, meta, take, weight, sens_half, small, choose, basx):
-            take = jnp.minimum(take, 2 * slots - 1)
-            index = source[:, : 2 * slots].reshape(4, slots, 2).transpose(0, 2, 1).reshape(-1)
-            return combined(slots, ident, index, meta, take, weight, tab, small, choose, line, basy, basx, flat, sens_half)
+        def branch(flat, plan, trajectory, phase_coef, sens):
+            return combined(slots, ident, plan, trajectory, phase_coef, tab, line, basy, basx, flat, sens)
 
         return branch
 
-    need = jnp.max(counts)
+    need = plan[8, 0]
     level = sum((need > 2 * s).astype(jnp.int32) for s in LEVELS[:-1])
-    return lax.switch(
-        level, [run(i, s) for i, s in enumerate(LEVELS)], flat, source, meta, take, weight, sens_half, small, choose, basx
-    )
+    return lax.switch(level, [run(i, s) for i, s in enumerate(LEVELS)], flat, plan, trajectory, phase_coef, sens)
 
 
 def solution(mesh):

time: 117 us -> 109 us (0.932)
  local copies, waits for them, and re-layouts: 9.35 us -> 3.49 us
  other arithmetic: 3.7 us -> 0 us
  Pallas kernels: 100 us -> 103 us
  matrix products: 1.74 us -> 0 us
    pallas_call x1 -> x2, Pallas kernels: 100 us -> 103 us  [the longest x1 101 us: combined(): pl.pallas_call(functools.partial(kernel, slots), in_specs=[sm] + [vm] * 6...]
    dynamic_slice x4 -> x0, local copies, waits for them, and re-layouts: 2.78 us -> none  [the longest x1 1.66 us: on_device(): basx = lax.dynamic_slice_in_dim(basx, half * HALF, HALF, 2)]
    dot_general x2 -> x0, matrix products: 1.74 us -> none  [the longest x1 0.89 us: on_device(): jnp.dot(kept.astype(F32), jnp.asarray(upto), preferred_element_type=F32)]
    another operation x16 -> x0, local copies, waits for them, and re-layouts: 1.51 us -> none
    convert_element_type x3 -> x0, other arithmetic: 1.4 us -> none  [the longest x1 0.69 us: on_device(): lax.dynamic_index_in_dim(trajectory, core, 0, False).astype(F32)]
    unnamed x1 -> x2, local copies, waits for them, and re-layouts: 1.57 us -> 2.95 us
where the time goes in v5:
time: 109 us; the launch traced here: 108 us
  Pallas kernels  103 us (94%)
  local copies, waits for them, and re-layouts  3.49 us (3%)
  between operations  1.31 us (1%)
    pallas_call x1, Pallas kernels, combined(): pl.pallas_call(functools.partial(kernel, slots), in_specs=[sm] + [vm] * 6...  101 us
    unnamed x2, local copies, waits for them, and re-layouts  2.95 us

profile of v5, /device:TPU:1, one launch (start us, length us, event | category | flops | bytes accessed | tf_op | source)
XLA Modules:
  0.0 108.4 jit_solution(6220475369651291212)
XLA Ops:
  0.0 1.4 %copy.52.accept_ref = s32[64,8]{1,0:T(8,128)} copy(s32[64,8]{0,1:T(8,128)} %param.13) | data formatting | bytes 4096 | tf_op args[1]
  1.4 1.6 %plan.1 = s32[16,128]{1,0:T(8,128)S(1)} custom-call(s32[64,8]{1,0:T(8,128)} %copy.52.accept_ref), custom_call_target="tpu_custom_call" | custom-call | tf_op jit(solution)/shard_map/plan/pallas_call | solution.py:459
  3.0 0.5 slice.4
  4.8 102.0 %conditional.1 = (f32[2,32,512]{2,1,0:T(8,128)}) conditional(s32[]{:T(128)} %bitcast, (s32[16,128]{1,0:T(8,128)S(1)}, s32[2,8,128]{2,1,0:T(8,128)}, f32[2,8,16,16]{3,2,1,0:T(8,128)}, bf16[512,512]{1,0:T(8,128)(2,1)}, bf16[2,256,256]{2,1,0:T(8,128)(2,1)}, /*index=5*/bf16[64,8,4,4,512]{4,3,2,1,0:T(4,128)(2,1)}, ...), branch_computations={%region_0.0_spmd.clone, %region_1.0_spmd.clone, %region_2.0_spmd.c... | conditional | flops 25769803776 | bytes 16777224 | solution.py:479
  5.1 101.3 %combined.4 = f32[2,32,512]{2,1,0:T(8,128)} custom-call(s32[16,128]{1,0:T(8,128)S(1)} %get-tuple-element.144.plan_ref, s32[2,8,128]{2,1,0:T(8,128)} %get-tuple-element.147.traj_ref, f32[2,8,16,16]{3,2,1,0:T(8,128)} %get-tuple-element.148.coef_ref, bf16[512,512]{1,0:T(8,128)(2,1)} %get-tuple-element.145.tab_ref, ...), custom_call_target="tpu_custom_call" | custom-call | flops 19327352832 | bytes 16777216 | tf_op jit(solution)/shard_map/cond/branch_1_fun/combined/pallas_call | solution.py:364
  106.8 1.6 %copy.57 = f32[2,32,512]{2,1,0:T(8,128)} copy(f32[2,32,512]{2,1,0:T(8,128)} %get-tuple-element.90) | data formatting | bytes 262144

commit v6 on v5

--- a/solution.py
+++ b/solution.py
@@ -98,8 +98,11 @@
     src = half * 2 + zl
     part = slots // CHUNKS
 
-    load = pltpu.make_async_copy(kspace_ref, kv, load_sem)
-    load.start()
+    loads = [
+        pltpu.make_async_copy(kspace_ref.at[k * 64:(k + 1) * 64], kv.at[k * 64:(k + 1) * 64], load_sem.at[k]) for k in range(8)
+    ]
+    for copy in loads:
+        copy.start()
     sens_parts = [
         (sens_ref.at[:, :, pl.ds(pl.multiple_of(k * IMG + half * HALF, HALF), HALF)], both.at[core, :, :, k * HALF:(k + 1) * HALF])
         for k in range(2)
@@ -129,6 +132,13 @@
     shifts = [(dz, (dz + t) % 4, dc) for t in range(4) for dz in range(4) for dc in range(2)]
     core_peer = (zh, zl, x, y, 1 - core)
 
+    barrier = pltpu.get_barrier_semaphore()
+    for _, p, bits in every:
+        pl.semaphore_signal(barrier, inc=1, device_id=target(p, bits), device_id_type=MESH)
+    for shift in shifts[1:]:
+        pl.semaphore_signal(barrier, inc=1, device_id=far(*shift), device_id_type=MESH)
+    for r in (1, 3):
+        pl.semaphore_signal(barrier, inc=1, device_id=along(r), device_id_type=MESH)
     small[0:SHOTS] = traj_ref[core].astype(F32)
     term = lax.broadcasted_iota(jnp.int32, (PB, 128), 0)
     place_lane = lax.broadcasted_iota(jnp.int32, (PB, 128), 1)
@@ -139,13 +149,6 @@
         spread_out = moved if spread_out is None else spread_out + moved
     small[SHOTS:] = spread_out
 
-    barrier = pltpu.get_barrier_semaphore()
-    for _, p, bits in every:
-        pl.semaphore_signal(barrier, inc=1, device_id=target(p, bits), device_id_type=MESH)
-    for shift in shifts[1:]:
-        pl.semaphore_signal(barrier, inc=1, device_id=far(*shift), device_id_type=MESH)
-    for r in (1, 3):
-        pl.semaphore_signal(barrier, inc=1, device_id=along(r), device_id_type=MESH)
     pl.semaphore_wait(barrier, len(every) + len(shifts) - 1 + 2)
 
     def remote(src_ref, dst_ref, sems, n, where):
@@ -177,7 +180,8 @@
     def self_copy(c, p):
         return pltpu.make_async_copy(send.at[4 + p, half, piece(c)], recv.at[p, src, core, piece(c)], self_sem.at[p, c])
 
-    load.wait()
+    for copy in loads:
+        copy.wait()
 
     def transform(c, carry):
         def one_group(g, carry):
@@ -206,7 +210,9 @@
     scale = 1.0 / (math.sqrt(128.0) * SHOTS)
     for s in range(2):
         for c in range(4):
-            sens[s, :, c * YB:(c + 1) * YB, :] = (both[s, c].astype(F32) * scale).reshape(4, YB, IMG)
+            real, imag = both[s, c, :, :HALF].astype(F32) * scale, both[s, c, :, HALF:].astype(F32) * scale
+            for k, values in enumerate((real, real - imag, real + imag)):
+                sens[s, k, :, c * YB:(c + 1) * YB] = values.reshape(4, YB, HALF)
     k = lax.broadcasted_iota(jnp.int32, (1, 128), 1)
     wx, wz = lax.rem(k // 32, 2), lax.rem(k // 16, 2)
     line_numbers = gath[:, :SHOTS, :].reshape(128, 128).astype(BF)
@@ -251,17 +257,15 @@
         for b in range(IMG // YB):
             turns = jnp.dot(basy_ref[b * YB:(b + 1) * YB, :], mixed6, preferred_element_type=F32)
             sine, cosine = sincos_turns(turns)
-            ure = uim = None
+            sums = None
             for s in range(2):
                 image = jnp.dot(weights[b], rhs[s], preferred_element_type=F32)
                 for c in range(4):
                     ire, iim = image[c * YB:(c + 1) * YB, :HALF], image[c * YB:(c + 1) * YB, HALF:]
-                    sre = sens[s, b, c * YB:(c + 1) * YB, :HALF]
-                    sim = sens[s, b, c * YB:(c + 1) * YB, HALF:]
-                    re = sre * ire + sim * iim
-                    im = sre * iim - sim * ire
-                    ure = re if ure is None else ure + re
-                    uim = im if uim is None else uim + im
+                    rows = slice(c * YB, (c + 1) * YB)
+                    terms = (ire + iim) * sens[s, 0, b, rows], iim * sens[s, 1, b, rows], ire * sens[s, 2, b, rows]
+                    sums = terms if sums is None else tuple(u + v for u, v in zip(sums, terms))
+            ure, uim = sums[0] - sums[1], sums[0] - sums[2]
             contrib[j, b, :, :HALF] = cosine * ure + sine * uim
             contrib[j, b, :, HALF:] = cosine * uim - sine * ure
 
@@ -374,7 +378,7 @@
             pltpu.VMEM((2, 4, IMG, IMG), BF),
             pltpu.VMEM((16, 24, 128), F32),
             pltpu.VMEM((2 * slots, 4, YB, IMG), F32),
-            pltpu.VMEM((2, 4, 4 * YB, IMG), F32),
+            pltpu.VMEM((2, 3, 4, 4 * YB, HALF), F32),
             pltpu.VMEM((4, 4 * YB, HALF), BF),
             pltpu.VMEM((4, 4 * YB, HALF), BF),
             pltpu.VMEM((256, 1, 128), F32),
@@ -385,7 +389,7 @@
             pltpu.VMEM((4, 2, 4, YB, IMG), BF),
             pltpu.VMEM((64, 32, IMG), BF),
             pltpu.VMEM((32, 32, IMG), BF),
-            dma,
+            dma((8,)),
             dma((2,)),
             dma((2, CHUNKS)),
             dma((14, CHUNKS)),

time: 109 us -> 108 us (level)
  no operation moved by 1% of the time
where the time goes in v6:
time: 108 us
  Pallas kernels  102 us (94%)
  local copies, waits for them, and re-layouts  3.49 us (3%)
  between operations  1.31 us (1%)
    pallas_call x1, Pallas kernels, combined(): pl.pallas_call(functools.partial(kernel, slots), in_specs=[sm] + [vm] * 6...  101 us
    unnamed x2, local copies, waits for them, and re-layouts  2.95 us

profile of v6, /device:TPU:1, one launch (start us, length us, event | category | flops | bytes accessed | tf_op | source)
XLA Modules:
  0.0 107.7 jit_solution(1942818241657814505)
XLA Ops:
  0.0 1.4 %copy.52.accept_ref = s32[64,8]{1,0:T(8,128)} copy(s32[64,8]{0,1:T(8,128)} %param.13) | data formatting | bytes 4096 | tf_op args[1]
  1.4 1.6 %plan.1 = s32[16,128]{1,0:T(8,128)S(1)} custom-call(s32[64,8]{1,0:T(8,128)} %copy.52.accept_ref), custom_call_target="tpu_custom_call" | custom-call | tf_op jit(solution)/shard_map/plan/pallas_call | solution.py:463
  3.0 0.5 slice.4
  4.8 101.2 %conditional.1 = (f32[2,32,512]{2,1,0:T(8,128)}) conditional(s32[]{:T(128)} %bitcast, (s32[16,128]{1,0:T(8,128)S(1)}, s32[2,8,128]{2,1,0:T(8,128)}, f32[2,8,16,16]{3,2,1,0:T(8,128)}, bf16[512,512]{1,0:T(8,128)(2,1)}, bf16[2,256,256]{2,1,0:T(8,128)(2,1)}, /*index=5*/bf16[64,8,4,4,512]{4,3,2,1,0:T(4,128)(2,1)}, ...), branch_computations={%region_0.0_spmd.clone, %region_1.0_spmd.clone, %region_2.0_spmd.c... | conditional | flops 25769803776 | bytes 16777224 | solution.py:483
  5.1 100.6 %combined.4 = f32[2,32,512]{2,1,0:T(8,128)} custom-call(s32[16,128]{1,0:T(8,128)S(1)} %get-tuple-element.144.plan_ref, s32[2,8,128]{2,1,0:T(8,128)} %get-tuple-element.147.traj_ref, f32[2,8,16,16]{3,2,1,0:T(8,128)} %get-tuple-element.148.coef_ref, bf16[512,512]{1,0:T(8,128)(2,1)} %get-tuple-element.145.tab_ref, ...), custom_call_target="tpu_custom_call" | custom-call | flops 19327352832 | bytes 16777216 | tf_op jit(solution)/shard_map/cond/branch_1_fun/combined/pallas_call | solution.py:368
  106.1 1.6 %copy.57 = f32[2,32,512]{2,1,0:T(8,128)} copy(f32[2,32,512]{2,1,0:T(8,128)} %get-tuple-element.90) | data formatting | bytes 262144
